TPU v7x, 256 devices: a whole 4x4x8 slice. The times are simulated.
256 devices in a mesh: gx: 4 (over x), gy: 4 (over y_lo, core), zt: 16 (over y_hi, z).
Axes of the slice: x: 4, y: 4 (y_hi: 2, y_lo: 2; y = y_hi * 2 + y_lo), z: 8, core: 2. Of those that a mesh axis runs over, the one named last changes fastest.
Arguments:
- gauge_links: float32 [4, 2, 3, 3, 8, 32, 2048], P(None, None, None, None, 'gx', 'gy', 'zt'), may hold values from -1 to 1, as said below
- momenta: float32 [4, 2, 3, 3, 8, 32, 2048], P(None, None, None, None, 'gx', 'gy', 'zt'), may hold values from -4 to 4, as said below
Outputs:
- new_links: float32 [4, 2, 3, 3, 8, 32, 2048], P(None, None, None, None, 'gx', 'gy', 'zt')
- new_momenta: float32 [4, 2, 3, 3, 8, 32, 2048], P(None, None, None, None, 'gx', 'gy', 'zt')
- plaquette: float32 [], replicated
Inputs may be any that keep to these rules, and one draw needn't show every extreme that they name: `gauge_links`: every link is a unitary 3 x 3 complex matrix. `momenta`: every momentum is an antihermitian traceless 3 x 3 complex matrix.
All inputs are finite; a program needn't handle non-finite values.
Results may differ from a plain program's by a relative error of at most 0.0001.
Values sent between devices are 32-bit elements; how exact they have to be, the bound alone decides.
No kernel may reach another device: no remote copies, remote signals or barrier semaphores. Data moves between devices by JAX's collectives and lax.ppermute only.
A program may use at most 128 MiB of HBM per device.

v0:
```python
import jax
import jax.numpy as jnp
from jax import lax
from jax.experimental import pallas as pl
from jax.experimental.pallas import tpu as pltpu
from jax.sharding import PartitionSpec as P


LT = 64
kick_size = 0.25
step_size = 0.2
OFF = ((0, 1), (0, 2), (1, 2))
PAIRS = tuple((m, n) for m in range(4) for n in range(m + 1, 4))
F32 = jnp.float32


def others(d):
    return tuple(m for m in range(4) if m != d)


def slot(d, m):
    return others(d).index(m)


def entry(a, b, i, j, ah, bh, want_re=True, want_im=True):
    re = im = None
    for k in range(3):
        ar, ai = a[k][i] if ah else a[i][k]
        br, bi = b[j][k] if bh else b[k][j]
        if want_re:
            t1, t2 = ar * br, ai * bi
            t = t1 + t2 if ah != bh else t1 - t2
            re = t if re is None else re + t
        if want_im:
            u1, u2 = ar * bi, ai * br
            if not ah and not bh:
                u = u1 + u2
            elif ah and not bh:
                u = u1 - u2
            elif bh and not ah:
                u = u2 - u1
            else:
                u = -(u1 + u2)
            im = u if im is None else im + u
    return (re, im)


def product(a, b, ah=False, bh=False):
    return [[entry(a, b, i, j, ah, bh) for j in range(3)] for i in range(3)]


def traceless(a):
    out = []
    for i, j in OFF:
        out.append(0.5 * (a[i][j][0] - a[j][i][0]))
        out.append(0.5 * (a[i][j][1] + a[j][i][1]))
    third = (a[0][0][1] + a[1][1][1] + a[2][2][1]) * (1.0 / 3.0)
    out.append(a[0][0][1] - third)
    out.append(a[1][1][1] - third)
    return out


def cayley(h):
    half = 0.5 * step_size
    x = [half * v for v in h]
    r01, i01, r02, i02, r12, i12, d0, d1 = x
    d2 = -(d0 + d1)
    n01 = r01 * r01 + i01 * i01
    n02 = r02 * r02 + i02 * i02
    n12 = r12 * r12 + i12 * i12
    s0 = -(d0 * d0 + n01 + n02)
    s1 = -(d1 * d1 + n01 + n12)
    s2 = -(d2 * d2 + n02 + n12)
    q = -0.5 * (s0 + s1 + s2)
    a01r = -(d0 + d1) * i01 - (r02 * r12 + i02 * i12)
    a01i = (d0 + d1) * r01 - (i02 * r12 - r02 * i12)
    a02r = -(d0 + d2) * i02 + (r01 * r12 - i01 * i12)
    a02i = (d0 + d2) * r02 + (r01 * i12 + i01 * r12)
    a12r = -(d1 + d2) * i12 - (r01 * r02 + i01 * i02)
    a12i = (d1 + d2) * r12 - (r01 * i02 - i01 * r02)
    delta = (
        -d0 * d1 * d2
        + d0 * n12
        + d1 * n02
        + d2 * n01
        + 2.0 * ((r01 * r12 - i01 * i12) * i02 - (r01 * i12 + i01 * r12) * r02)
    )
    w = 1.0 + q
    inv = 1.0 / (w * w + delta * delta)
    fr, fi = w * inv, delta * inv

    def scaled(re, im):
        return (re * fr - im * fi, re * fi + im * fr)

    m = [[None] * 3 for _ in range(3)]
    for (i, j), (hr, hi), (xr, xi) in (
        ((0, 1), (a01r, a01i), (r01, i01)),
        ((0, 2), (a02r, a02i), (r02, i02)),
        ((1, 2), (a12r, a12i), (r12, i12)),
    ):
        m[i][j] = scaled(2.0 * (hr + xr), 2.0 * (hi + xi))
        m[j][i] = scaled(2.0 * (hr - xr), 2.0 * (xi - hi))
    for i, s, d in ((0, s0, d0), (1, s1, d1), (2, s2, d2)):
        m[i][i] = scaled(2.0 * s + w, 2.0 * d + delta)
    return m


def lane_of():
    return lax.broadcasted_iota(jnp.int32, (8, 128), 1)


def row_of():
    return lax.broadcasted_iota(jnp.int32, (8, 128), 0)


def load_link(ref, m, x):
    return [[(ref[m, 0, i, j, x], ref[m, 1, i, j, x]) for j in range(3)] for i in range(3)]


def comp(ri, i, j):
    return ri * 9 + i * 3 + j


class Ahead:
    def __init__(self, ref, xh, yh, zh):
        self.ref, self.xh, self.yh, self.zh = ref, xh, yh, zh
        self.lane, self.row = lane_of(), row_of()

    def one(self, n, d, x, ri, i, j):
        c = comp(ri, i, j)
        k = slot(d, n)
        if d == 0:
            return self.ref[n, ri, i, j, 1] if x == 0 else self.xh[k * 18 + c]
        v = self.ref[n, ri, i, j, x]
        if d == 1:
            halo = jnp.broadcast_to(self.yh[c, pl.ds(2 * k + x, 1), :], (8, 128))
            return jnp.where(self.row == 7, halo, pltpu.roll(v, 7, 0))
        if d == 2:
            h = self.zh[k * 18 + c]
            if x == 0:
                return pltpu.roll(jnp.where(self.lane < LT, h, v), LT, 1)
            return jnp.where(self.lane < LT, pltpu.roll(v, LT, 1), h)
        return jnp.where((self.lane & (LT - 1)) == LT - 1, pltpu.roll(v, LT - 1, 1), pltpu.roll(v, 127, 1))

    def __call__(self, n, d, x):
        return [[(self.one(n, d, x, 0, i, j), self.one(n, d, x, 1, i, j)) for j in range(3)] for i in range(3)]


def pack_z(a, b):
    return jnp.where(lane_of() < LT, a, pltpu.roll(b, LT, 1))


def cross(a, k):
    i, j = (k + 1) % 3, (k + 2) % 3
    (pr, pi), (qr, qi) = a[0][i], a[1][j]
    (rr, ri), (sr, si) = a[0][j], a[1][i]
    return (pr * qr - pi * qi - rr * sr + ri * si, pr * qi + pi * qr - rr * si - ri * sr)


def store_short(ref, base, a):
    dr = di = None
    for k in range(3):
        cr, ci = cross(a, k)
        vr, vi = a[2][k]
        tr, ti = vr * cr - vi * ci, vr * ci + vi * cr
        dr, di = (tr, ti) if dr is None else (dr + tr, di + ti)
    for i in range(2):
        for k in range(3):
            ref[base + 2 * (3 * i + k)] = a[i][k][0]
            ref[base + 2 * (3 * i + k) + 1] = a[i][k][1]
    ref[base + 12] = dr
    ref[base + 13] = di


def load_short(ref, base):
    a = [[(ref[base + 2 * (3 * i + k)], ref[base + 2 * (3 * i + k) + 1]) for k in range(3)] for i in range(2)]
    dr, di = ref[base + 12], ref[base + 13]
    last = []
    for k in range(3):
        cr, ci = cross(a, k)
        last.append((dr * cr + di * ci, di * cr - dr * ci))
    return [*a, last]


def store_flat(ref, base, a):
    for i in range(3):
        for j in range(3):
            ref[base + comp(0, i, j)] = a[i][j][0]
            ref[base + comp(1, i, j)] = a[i][j][1]


def load_flat(ref, base):
    return [[(ref[base + comp(0, i, j)], ref[base + comp(1, i, j)]) for j in range(3)] for i in range(3)]


def pack_kernel(v, xs, ys, zs, rows):
    for n in range(4):
        if n != 0:
            store_short(xs, slot(0, n) * 14, load_link(v, n, 0))
        if n != 1:
            k = slot(1, n)
            for ri in range(2):
                for i in range(3):
                    for j in range(3):
                        for x in range(2):
                            rows[comp(ri, i, j), pl.ds(2 * k + x, 1), :] = v[n, ri, i, j, x, 0:1, :]
        if n != 2:
            a, b = load_link(v, n, 0), load_link(v, n, 1)
            z = [[tuple(pack_z(a[i][j][r], b[i][j][r]) for r in range(2)) for j in range(3)] for i in range(3)]
            store_short(zs, slot(2, n) * 14, z)
    for c in range(18):
        rows[c, 6:8, :] = jnp.zeros((2, 128), F32)
    store_short(ys, 0, load_flat(rows, 0))


class Force:
    def __init__(self, f, xs, ys, zs):
        self.f, self.xs, self.ys, self.zs = f, xs, ys, zs
        self.lane, self.row = lane_of(), row_of()
        self.seen = set()

    def put(self, m, c, x, w, minus):
        if (m, c, x) in self.seen:
            self.f[m, c, x] = self.f[m, c, x] - w if minus else self.f[m, c, x] + w
        else:
            self.seen.add((m, c, x))
            self.f[m, c, x] = -w if minus else w

    def ahead(self, m, d, x, t, minus):
        k = slot(d, m) if d < 3 else None
        for c in range(8):
            w = t[c]
            if d == 0:
                if x == 0:
                    self.put(m, c, 1, w, minus)
                else:
                    self.xs[k * 8 + c] = -w if minus else w
            elif d == 1:
                self.ys[c, pl.ds(2 * k + x, 1), :] = (-w if minus else w)[7:8, :]
                self.put(m, c, x, jnp.where(self.row == 0, 0.0, pltpu.roll(w, 1, 0)), minus)
            elif d == 2:
                r = pltpu.roll(w, LT, 1)
                self.put(m, c, x, jnp.where(self.lane < LT, 0.0, r), minus)
                if x == 0:
                    self.zs[k * 8 + c] = -r if minus else r
                else:
                    self.zs[k * 8 + c] = jnp.where(self.lane < LT, self.zs[k * 8 + c], -w if minus else w)
            else:
                r = jnp.where((self.lane & (LT - 1)) == 0, pltpu.roll(w, LT + 1, 1), pltpu.roll(w, 1, 1))
                self.put(m, c, x, r, minus)


def corner(ahead, m, n, x):
    return product(ahead(n, m, x), ahead(m, n, x), bh=True)


def load_pair(ref, m, n, x):
    p = PAIRS.index((m, n))
    return [[(ref[p, 0, i, j, x], ref[p, 1, i, j, x]) for j in range(3)] for i in range(3)]


def store_pair(ref, m, n, x, a):
    p = PAIRS.index((m, n))
    for i in range(3):
        for j in range(3):
            ref[p, 0, i, j, x] = a[i][j][0]
            ref[p, 1, i, j, x] = a[i][j][1]


def local_kernel(v, out):
    for m, n in PAIRS:
        for x in range(2):
            store_pair(out, m, n, x, product(load_link(v, n, x), load_link(v, m, x), ah=True))


def add_shifted(force, a, m, n, x, c):
    force.ahead(m, n, x, traceless(product(a, c)), True)
    force.ahead(n, m, x, traceless(product(c, a)), False)


def add_upper(links, corners, f, out):
    out[...] = f[...]
    for m, n in PAIRS:
        for x in range(2):
            vm, vn = load_link(links, m, x), load_link(links, n, x)
            t = traceless(product(product(vm, load_pair(corners, m, n, x)), vn, bh=True))
            for c in range(8):
                out[m, c, x] = out[m, c, x] + t[c]
                out[n, c, x] = out[n, c, x] - t[c]


def clear_rows(ys):
    for c in range(8):
        ys[c, 6:8, :] = jnp.zeros((2, 128), F32)


def force_kernel(v, a, xh, yh, zh, f, xs, ys, zs, xw, yw, zw, corners):
    clear_rows(ys)
    for short, whole, count in ((xh, xw, 3), (yh, yw, 1), (zh, zw, 3)):
        for k in range(count):
            store_flat(whole, 18 * k, load_short(short, 14 * k))
    ahead = Ahead(v, xw, yw, zw)
    force = Force(f, xs, ys, zs)
    for m, n in PAIRS:
        for x in range(2):
            c = corner(ahead, m, n, x)
            store_pair(corners, m, n, x, c)
            add_shifted(force, load_pair(a, m, n, x), m, n, x, c)


def upper_kernel(v, corners, f, out):
    add_upper(v, corners, f, out)


def arrived(xr, yr, zr, m, c, x):
    total = None
    if m != 0 and x == 0:
        total = xr[slot(0, m) * 8 + c]
    if m != 1:
        w = jnp.broadcast_to(yr[c, pl.ds(2 * slot(1, m) + x, 1), :], (8, 128))
        w = jnp.where(row_of() == 0, w, 0.0)
        total = w if total is None else total + w
    if m != 2:
        w = zr[slot(2, m) * 8 + c]
        if x == 1:
            w = pltpu.roll(w, LT, 1)
        w = jnp.where(lane_of() < LT, w, 0.0)
        total = w if total is None else total + w
    return total


def momentum_part(ref, m, c, x):
    if c < 6:
        i, j = OFF[c // 2]
        return ref[m, c % 2, i, j, x]
    return ref[m, 1, c - 6, c - 6, x]


def half_kernel(p, f, xr, yr, zr, h, xs, ys, zs):
    for c in range(8):
        ys[c, 6:8, :] = jnp.zeros((2, 128), F32)
        for m in range(4):
            v = []
            for x in range(2):
                g = f[m, c, x] + arrived(xr, yr, zr, m, c, x)
                v.append(momentum_part(p, m, c, x) - kick_size * g)
                h[m, c, x] = v[x]
                if m != 1:
                    ys[c, pl.ds(2 * slot(1, m) + x, 1), :] = v[x][0:1, :]
            if m != 0:
                xs[slot(0, m) * 8 + c] = v[0]
            if m != 2:
                zs[slot(2, m) * 8 + c] = pack_z(v[0], v[1])


def link_kernel(v, h, out):
    for m in range(4):
        for x in range(2):
            new = product(cayley([h[m, c, x] for c in range(8)]), load_link(v, m, x))
            for i in range(3):
                for j in range(3):
                    out[m, 0, i, j, x] = new[i][j][0]
                    out[m, 1, i, j, x] = new[i][j][1]


def corner_kernel(v, a, xh, yh, zh, xm, ym, zm, corners, trace, nx, ny, nz):
    for old, mom, new, count in ((xh, xm, nx, 3), (yh, ym, ny, 1), (zh, zm, nz, 3)):
        for k in range(count):
            store_flat(new, 18 * k, product(cayley([mom[k * 8 + c] for c in range(8)]), load_flat(old, 18 * k)))
    ahead = Ahead(v, nx, ny, nz)
    total = None
    for m, n in PAIRS:
        for x in range(2):
            c = corner(ahead, m, n, x)
            store_pair(corners, m, n, x, c)
            b = load_pair(a, m, n, x)
            for i in range(3):
                t = entry(c, b, i, i, False, False, want_im=False)[0]
                total = t if total is None else total + t
    trace[...] = jnp.broadcast_to(jnp.sum(total, axis=0, keepdims=True), trace.shape)


def second_kernel(a, corners, f, xs, ys, zs):
    clear_rows(ys)
    force = Force(f, xs, ys, zs)
    for m, n in PAIRS:
        for x in range(2):
            add_shifted(force, load_pair(a, m, n, x), m, n, x, load_pair(corners, m, n, x))


def final_kernel(v, corners, f, out, links):
    links[...] = v[...]
    add_upper(v, corners, f, out)


def last_kernel(h, f, xr, yr, zr, traces, out, plaquette):
    total = jnp.sum(traces[...], axis=0, keepdims=True)
    plaquette[...] = jnp.sum(total, axis=1, keepdims=True) * (4.0 / (72.0 * 2 * 8 * 128 * traces.shape[0]))
    for m in range(4):
        for x in range(2):
            u = [h[m, c, x] - kick_size * (f[m, c, x] + arrived(xr, yr, zr, m, c, x)) for c in range(8)]
            for k, (i, j) in enumerate(OFF):
                out[m, 0, i, j, x] = u[2 * k]
                out[m, 0, j, i, x] = -u[2 * k]
                out[m, 1, i, j, x] = u[2 * k + 1]
                out[m, 1, j, i, x] = u[2 * k + 1]
            for i, d in enumerate((u[6], u[7], -(u[6] + u[7]))):
                out[m, 0, i, i, x] = jnp.zeros((8, 128), F32)
                out[m, 1, i, i, x] = d


def call(kernel, shapes, flops, scratch=()):
    def run(*args):
        vmem = pl.BlockSpec(memory_space=pltpu.VMEM)
        return pl.pallas_call(
            kernel,
            out_shape=[jax.ShapeDtypeStruct(s, F32) for s in shapes],
            in_specs=[vmem] * len(args),
            out_specs=[vmem] * len(shapes),
            scratch_shapes=[pltpu.VMEM(s, F32) for s in scratch],
            cost_estimate=pl.CostEstimate(flops=flops, bytes_accessed=2_000_000, transcendentals=0),
            compiler_params=pltpu.CompilerParams(vmem_limit_bytes=VMEM_LIMIT),
        )(*args)

    return run


LINK = (4, 2, 3, 3, 2, 8, 128)
HALO_LINK = ((54, 8, 128), (18, 8, 128), (54, 8, 128))
HALO_SHORT = ((42, 8, 128), (14, 8, 128), (42, 8, 128))
HALO_MOM = ((24, 8, 128), (8, 8, 128), (24, 8, 128))
MOM = (4, 8, 2, 8, 128)
CORNER = (6, 2, 3, 3, 2, 8, 128)
BIG = 400_000_000
VMEM_LIMIT = 16 * 1024 * 1024


def solution(mesh):
    size = dict(mesh.shape)

    def shift(a, axis, step):
        n = size[axis]
        return lax.ppermute(a, axis, [(i, (i + step) % n) for i in range(n)])

    def halos(arrays, step):
        return [shift(a, axis, step) for a, axis in zip(arrays, ("gx", "gy", "zt"), strict=True)]

    def body(v, p):
        halo = halos(call(pack_kernel, HALO_SHORT, 1_000_000, ((18, 8, 128),))(v), -1)
        (a,) = call(local_kernel, (CORNER,), 100_000_000)(v)
        f, *up = call(force_kernel, (MOM, *HALO_MOM, *HALO_LINK, CORNER), BIG)(v, a, *halo)
        up, halo, corners = up[:3], up[3:6], up[6]
        up = halos(up, 1)
        (f,) = call(upper_kernel, (MOM,), 100_000_000)(v, corners, f)
        h, *down = call(half_kernel, (MOM, *HALO_MOM), 1_000_000)(p, f, *up)
        down = halos(down, -1)
        (new,) = call(link_kernel, (LINK,), 100_000_000)(v, h)
        (a,) = call(local_kernel, (CORNER,), 100_000_000)(new)
        corners, trace = call(corner_kernel, (CORNER, (mesh.size, 128)), 100_000_000, HALO_LINK)(new, a, *halo, *down)
        traces = lax.all_to_all(trace, mesh.axis_names, split_axis=0, concat_axis=0, tiled=True)
        f, *up = call(second_kernel, (MOM, *HALO_MOM), 100_000_000)(a, corners)
        up = halos(up, 1)
        f, new = call(final_kernel, (MOM, LINK), 100_000_000)(new, corners, f)
        last, plaquette = call(last_kernel, (LINK, (1, 1)), 1_000_000)(h, f, *up, traces)
        return new, last, plaquette.reshape(())

    spec = P(None, None, None, None, "gx", "gy", "zt")
    return jax.shard_map(body, mesh=mesh, in_specs=(spec, spec), out_specs=(spec, spec, P()), check_vma=False)
```

profile of v0, /device:TPU:1, one launch (start us, length us, event | category | flops | bytes accessed | tf_op | source)
XLA Modules:
  0.0 59.3 jit_solution(9913533509106394235)
XLA Ops:
  0.6 1.1 %copy-done = f32[4,2,3,3,2,8,128]{6,5,4,3,2,1,0:T(8,128)S(1)} copy-done((f32[4,2,3,3,2,8,128]{6,5,4,3,2,1,0:T(8,128)S(1)}, f32[4,2,3,3,2,8,128]{6,5,4,3,2,1,0:T(8,128)}, u32[]{:S(2)}) %copy-start) | copy-done | bytes 589848
  1.8 3.4 %collective-permute-start = (f32[42,8,128]{2,1,0:T(8,128)S(1)}, f32[42,8,128]{2,1,0:T(8,128)S(1)}, u32[]{:S(2)}, u32[]{:S(2)}) collective-permute-start(f32[42,8,128]{2,1,0:T(8,128)S(1)} %get-tuple-element.28), channel_id=1, source_target_pairs={{0,192},{64,0},{128,64},{192,128},{1,193},{65,1},{129,65},{193,129... | collective-permute-start | bytes 516104 | tf_op jit(solution)/shard_map/ppermute | solution.py:443
  5.2 8.2 %collective-permute-start.2 = (f32[42,8,128]{2,1,0:T(8,128)S(1)}, f32[42,8,128]{2,1,0:T(8,128)S(1)}, u32[]{:S(2)}, u32[]{:S(2)}) collective-permute-start(f32[42,8,128]{2,1,0:T(8,128)S(1)} %get-tuple-element.30), channel_id=1, source_target_pairs={{0,15},{1,0},{2,1},{3,2},{4,3},{5,4},{6,5},{7,6},{8,7},{9,8},{10,9... | collective-permute-start | bytes 516104 | tf_op jit(solution)/shard_map/ppermute | solution.py:443
  13.4 1.2 %collective-permute-start.1 = (f32[14,8,128]{2,1,0:T(8,128)S(1)}, f32[14,8,128]{2,1,0:T(8,128)S(1)}, u32[]{:S(2)}, u32[]{:S(2)}) collective-permute-start(f32[14,8,128]{2,1,0:T(8,128)S(1)} %get-tuple-element.29), channel_id=1, source_target_pairs={{0,48},{16,0},{32,16},{48,32},{1,49},{17,1},{33,17},{49,33},{2,50}... | collective-permute-start | bytes 172040 | tf_op jit(solution)/shard_map/ppermute | solution.py:443
  15.0 2.0 %collective-permute-done.1.yh = f32[14,8,128]{2,1,0:T(8,128)S(1)} collective-permute-done((f32[14,8,128]{2,1,0:T(8,128)S(1)}, f32[14,8,128]{2,1,0:T(8,128)S(1)}, u32[]{:S(2)}, u32[]{:S(2)}) %collective-permute-start.1) | collective-permute-done | bytes 57376 | tf_op jit(solution)/shard_map/ppermute | solution.py:443
  17.0 1.5 %shard_map.51 = (f32[4,8,2,8,128]{4,3,2,1,0:T(8,128)S(1)}, f32[24,8,128]{2,1,0:T(8,128)S(1)}, f32[8,8,128]{2,1,0:T(8,128)S(1)}, f32[24,8,128]{2,1,0:T(8,128)S(1)...) custom-call(f32[4,2,3,3,2,8,128]{6,5,4,3,2,1,0:T(8,128)S(1)} %copy-d, ...), custom_call_target="tpu_custom_call" | custom-call | flops 400000000 | bytes 2000000 | tf_op jit(solution)/shard_map/pallas_call | solution.py:415
  18.8 1.3 %collective-permute-start.4 = (f32[8,8,128]{2,1,0:T(8,128)S(1)}, f32[8,8,128]{2,1,0:T(8,128)S(1)}, u32[]{:S(2)}, u32[]{:S(2)}) collective-permute-start(f32[8,8,128]{2,1,0:T(8,128)S(1)} %get-tuple-element.34), channel_id=1, source_target_pairs={{0,16},{16,32},{32,48},{48,0},{1,17},{17,33},{33,49},{49,1},{2,18}... | collective-permute-start | bytes 98312 | tf_op jit(solution)/shard_map/ppermute | solution.py:443
  20.1 0.7 %shard_map.52.f = f32[4,8,2,8,128]{4,3,2,1,0:T(8,128)S(1)} custom-call(f32[4,2,3,3,2,8,128]{6,5,4,3,2,1,0:T(8,128)S(1)} %copy-done, f32[6,2,3,3,2,8,128]{6,5,4,3,2,1,0:T(8,128)S(1)} %get-tuple-element.31.corners, f32[4,8,2,8,128]{4,3,2,1,0:T(8,128)S(1)} %get-tuple-element.32.f), custom_call_target="tpu_custom_call" | custom-call | flops 100000000 | bytes 2000000 | tf_op jit(solution)/shard_map/pallas_call | solution.py:415
  21.1 2.2 %collective-permute-done.3.xr = f32[24,8,128]{2,1,0:T(8,128)S(1)} collective-permute-done((f32[24,8,128]{2,1,0:T(8,128)S(1)}, f32[24,8,128]{2,1,0:T(8,128)S(1)}, u32[]{:S(2)}, u32[]{:S(2)}) %collective-permute-start.3) | collective-permute-done | bytes 98336 | tf_op jit(solution)/shard_map/ppermute | solution.py:443
  23.3 2.5 %collective-permute-done.5.zr = f32[24,8,128]{2,1,0:T(8,128)S(1)} collective-permute-done((f32[24,8,128]{2,1,0:T(8,128)S(1)}, f32[24,8,128]{2,1,0:T(8,128)S(1)}, u32[]{:S(2)}, u32[]{:S(2)}) %collective-permute-start.5) | collective-permute-done | bytes 98336 | tf_op jit(solution)/shard_map/ppermute | solution.py:443
  26.0 2.7 %collective-permute-start.6 = (f32[24,8,128]{2,1,0:T(8,128)S(1)}, f32[24,8,128]{2,1,0:T(8,128)S(1)}, u32[]{:S(2)}, u32[]{:S(2)}) collective-permute-start(f32[24,8,128]{2,1,0:T(8,128)S(1)} %get-tuple-element.40), channel_id=1, source_target_pairs={{0,192},{64,0},{128,64},{192,128},{1,193},{65,1},{129,65},{193,129... | collective-permute-start | bytes 294920 | tf_op jit(solution)/shard_map/ppermute | solution.py:443
  28.7 1.9 %collective-permute-start.8 = (f32[24,8,128]{2,1,0:T(8,128)S(1)}, f32[24,8,128]{2,1,0:T(8,128)S(1)}, u32[]{:S(2)}, u32[]{:S(2)}) collective-permute-start(f32[24,8,128]{2,1,0:T(8,128)S(1)} %get-tuple-element.42), channel_id=1, source_target_pairs={{0,15},{1,0},{2,1},{3,2},{4,3},{5,4},{6,5},{7,6},{8,7},{9,8},{10,9... | collective-permute-start | bytes 294920 | tf_op jit(solution)/shard_map/ppermute | solution.py:443
  30.6 3.2 %collective-permute-start.7 = (f32[8,8,128]{2,1,0:T(8,128)S(1)}, f32[8,8,128]{2,1,0:T(8,128)S(1)}, u32[]{:S(2)}, u32[]{:S(2)}) collective-permute-start(f32[8,8,128]{2,1,0:T(8,128)S(1)} %get-tuple-element.41), channel_id=1, source_target_pairs={{0,48},{16,0},{32,16},{48,32},{1,49},{17,1},{33,17},{49,33},{2,50}... | collective-permute-start | bytes 98312 | tf_op jit(solution)/shard_map/ppermute | solution.py:443
  34.6 1.4 %collective-permute-done.7.ym = f32[8,8,128]{2,1,0:T(8,128)S(1)} collective-permute-done((f32[8,8,128]{2,1,0:T(8,128)S(1)}, f32[8,8,128]{2,1,0:T(8,128)S(1)}, u32[]{:S(2)}, u32[]{:S(2)}) %collective-permute-start.7) | collective-permute-done | bytes 32800 | tf_op jit(solution)/shard_map/ppermute | solution.py:443
  36.0 1.6 %shard_map.56 = (f32[6,2,3,3,2,8,128]{6,5,4,3,2,1,0:T(8,128)S(1)}, f32[256,128]{1,0:T(8,128)}) custom-call(f32[4,2,3,3,2,8,128]{6,5,4,3,2,1,0:T(8,128)S(1)} %shard_map.54.v, f32[6,2,3,3,2,8,128]{6,5,4,3,2,1,0:T(8,128)S(1)} %shard_map.55.a, f32[54,8,128]{2,1,0:T(8,128)S(1)} %get-tuple-element.37.xh, f32[18,8,128]{2,1,0:T(8,128)S(1)} %get-tuple-element.38.yh, ...), custom_call_target="tpu_custom_call" | custom-call | flops 100000000 | bytes 2000000 | tf_op jit(solution)/shard_map/pallas_call | solution.py:415
  37.6 7.9 %all-to-all-start = ((f32[256,1,128]{2,1,0:T(1,128)}), f32[256,1,128]{2,1,0:T(1,128)S(1)}, u32[]{:S(2)}, u32[]{:S(2)}) async-start(f32[256,1,128]{2,1,0:T(1,128)} %bitcast.1), calls=%async_computation | async-start | bytes 262144 | tf_op jit(solution)/shard_map/all_to_all | solution.py:460
  45.5 0.6 %shard_map.57 = (f32[4,8,2,8,128]{4,3,2,1,0:T(8,128)S(1)}, f32[24,8,128]{2,1,0:T(8,128)S(1)}, f32[8,8,128]{2,1,0:T(8,128)S(1)}, f32[24,8,128]{2,1,0:T(8,128)S(1)}) custom-call(f32[6,2,3,3,2,8,128]{6,5,4,3,2,1,0:T(8,128)S(1)} %shard_map.55.a, f32[6,2,3,3,2,8,128]{6,5,4,3,2,1,0:T(8,128)S(1)} %get-tuple-element.43.corners), custom_call_target="tpu_custom_call" | custom-call | flops 100000000 | bytes 2000000 | tf_op jit(solution)/shard_map/pallas_call | solution.py:415
  46.1 1.4 %collective-permute-start.9 = (f32[24,8,128]{2,1,0:T(8,128)S(1)}, f32[24,8,128]{2,1,0:T(8,128)S(1)}, u32[]{:S(2)}, u32[]{:S(2)}) collective-permute-start(f32[24,8,128]{2,1,0:T(8,128)S(1)} %get-tuple-element.47), channel_id=1, source_target_pairs={{0,64},{64,128},{128,192},{192,0},{1,65},{65,129},{129,193},{193,1... | collective-permute-start | bytes 294920 | tf_op jit(solution)/shard_map/ppermute | solution.py:443
  47.6 1.3 %collective-permute-start.11 = (f32[24,8,128]{2,1,0:T(8,128)S(1)}, f32[24,8,128]{2,1,0:T(8,128)S(1)}, u32[]{:S(2)}, u32[]{:S(2)}) collective-permute-start(f32[24,8,128]{2,1,0:T(8,128)S(1)} %get-tuple-element.49), channel_id=1, source_target_pairs={{0,1},{1,2},{2,3},{3,4},{4,5},{5,6},{6,7},{7,8},{8,9},{9,10},{10,1... | collective-permute-start | bytes 294920 | tf_op jit(solution)/shard_map/ppermute | solution.py:443
  48.9 2.1 %collective-permute-start.10 = (f32[8,8,128]{2,1,0:T(8,128)S(1)}, f32[8,8,128]{2,1,0:T(8,128)S(1)}, u32[]{:S(2)}, u32[]{:S(2)}) collective-permute-start(f32[8,8,128]{2,1,0:T(8,128)S(1)} %get-tuple-element.48), channel_id=1, source_target_pairs={{0,16},{16,32},{32,48},{48,0},{1,17},{17,33},{33,49},{49,1},{2,18}... | collective-permute-start | bytes 98312 | tf_op jit(solution)/shard_map/ppermute | solution.py:443
  51.0 0.9 %shard_map.58 = (f32[4,8,2,8,128]{4,3,2,1,0:T(8,128)S(1)}, f32[4,2,3,3,2,8,128]{6,5,4,3,2,1,0:T(8,128)}) custom-call(f32[4,2,3,3,2,8,128]{6,5,4,3,2,1,0:T(8,128)S(1)} %shard_map.54.v, f32[6,2,3,3,2,8,128]{6,5,4,3,2,1,0:T(8,128)S(1)} %get-tuple-element.43.corners, f32[4,8,2,8,128]{4,3,2,1,0:T(8,128)S(1)} %get-tuple-element.44.f), custom_call_target="tpu_custom_call" | custom-call | flops 100000000 | bytes 2000000 | tf_op jit(solution)/shard_map/pallas_call | solution.py:415
  52.0 5.1 %collective-permute-done.11.zr = f32[24,8,128]{2,1,0:T(8,128)S(1)} collective-permute-done((f32[24,8,128]{2,1,0:T(8,128)S(1)}, f32[24,8,128]{2,1,0:T(8,128)S(1)}, u32[]{:S(2)}, u32[]{:S(2)}) %collective-permute-start.11) | collective-permute-done | bytes 98336 | tf_op jit(solution)/shard_map/ppermute | solution.py:443
  57.1 1.3 %all-to-all-done = f32[256,1,128]{2,1,0:T(1,128)S(1)} async-done(((f32[256,1,128]{2,1,0:T(1,128)}), f32[256,1,128]{2,1,0:T(1,128)S(1)}, u32[]{:S(2)}, u32[]{:S(2)}) %all-to-all-start) | async-done | bytes 131104 | tf_op jit(solution)/shard_map/all_to_all | solution.py:460
  58.4 0.9 %shard_map.59 = (f32[4,2,3,3,2,8,128]{6,5,4,3,2,1,0:T(8,128)}, f32[1,1]{1,0:T(1,128)}) custom-call(f32[4,8,2,8,128]{4,3,2,1,0:T(8,128)S(1)} %get-tuple-element.36.h, f32[4,8,2,8,128]{4,3,2,1,0:T(8,128)S(1)} %get-tuple-element.46.f, f32[24,8,128]{2,1,0:T(8,128)S(1)} %collective-permute-done.9.xr, f32[8,8,128]{2,1,0:T(8,128)S(1)} %collective-permute-done.10.yr, ...), custom_call_target="tpu_custom_call" | custom-call | flops 1000000 | bytes 2000000 | tf_op jit(solution)/shard_map/pallas_call | solution.py:415
  (19 shorter events, 2.1 us)
Async XLA Ops:
  0.6 1.1 %copy-start = (f32[4,2,3,3,2,8,128]{6,5,4,3,2,1,0:T(8,128)S(1)}, f32[4,2,3,3,2,8,128]{6,5,4,3,2,1,0:T(8,128)}, u32[]{:S(2)}) copy-start(f32[4,2,3,3,2,8,128]{6,5,4,3,2,1,0:T(8,128)} %v.9) | copy-start | bytes 1769476
  1.8 15.2 %collective-permute-start = (f32[42,8,128]{2,1,0:T(8,128)S(1)}, f32[42,8,128]{2,1,0:T(8,128)S(1)}, u32[]{:S(2)}, u32[]{:S(2)}) collective-permute-start(f32[42,8,128]{2,1,0:T(8,128)S(1)} %get-tuple-element.28), channel_id=1, source_target_pairs={{0,192},{64,0},{128,64},{192,128},{1,193},{65,1},{129,65},{193,129... | collective-permute-start | bytes 516104 | tf_op jit(solution)/shard_map/ppermute | solution.py:443
  5.2 11.8 %collective-permute-start.2 = (f32[42,8,128]{2,1,0:T(8,128)S(1)}, f32[42,8,128]{2,1,0:T(8,128)S(1)}, u32[]{:S(2)}, u32[]{:S(2)}) collective-permute-start(f32[42,8,128]{2,1,0:T(8,128)S(1)} %get-tuple-element.30), channel_id=1, source_target_pairs={{0,15},{1,0},{2,1},{3,2},{4,3},{5,4},{6,5},{7,6},{8,7},{9,8},{10,9... | collective-permute-start | bytes 516104 | tf_op jit(solution)/shard_map/ppermute | solution.py:443
  13.4 3.6 %collective-permute-start.1 = (f32[14,8,128]{2,1,0:T(8,128)S(1)}, f32[14,8,128]{2,1,0:T(8,128)S(1)}, u32[]{:S(2)}, u32[]{:S(2)}) collective-permute-start(f32[14,8,128]{2,1,0:T(8,128)S(1)} %get-tuple-element.29), channel_id=1, source_target_pairs={{0,48},{16,0},{32,16},{48,32},{1,49},{17,1},{33,17},{49,33},{2,50}... | collective-permute-start | bytes 172040 | tf_op jit(solution)/shard_map/ppermute | solution.py:443
  18.6 4.8 %collective-permute-start.3 = (f32[24,8,128]{2,1,0:T(8,128)S(1)}, f32[24,8,128]{2,1,0:T(8,128)S(1)}, u32[]{:S(2)}, u32[]{:S(2)}) collective-permute-start(f32[24,8,128]{2,1,0:T(8,128)S(1)} %get-tuple-element.33), channel_id=1, source_target_pairs={{0,64},{64,128},{128,192},{192,0},{1,65},{65,129},{129,193},{193,1... | collective-permute-start | bytes 294920 | tf_op jit(solution)/shard_map/ppermute | solution.py:443
  18.7 7.2 %collective-permute-start.5 = (f32[24,8,128]{2,1,0:T(8,128)S(1)}, f32[24,8,128]{2,1,0:T(8,128)S(1)}, u32[]{:S(2)}, u32[]{:S(2)}) collective-permute-start(f32[24,8,128]{2,1,0:T(8,128)S(1)} %get-tuple-element.35), channel_id=1, source_target_pairs={{0,1},{1,2},{2,3},{3,4},{4,5},{5,6},{6,7},{7,8},{8,9},{9,10},{10,1... | collective-permute-start | bytes 294920 | tf_op jit(solution)/shard_map/ppermute | solution.py:443
  18.8 2.4 %collective-permute-start.4 = (f32[8,8,128]{2,1,0:T(8,128)S(1)}, f32[8,8,128]{2,1,0:T(8,128)S(1)}, u32[]{:S(2)}, u32[]{:S(2)}) collective-permute-start(f32[8,8,128]{2,1,0:T(8,128)S(1)} %get-tuple-element.34), channel_id=1, source_target_pairs={{0,16},{16,32},{32,48},{48,0},{1,17},{17,33},{33,49},{49,1},{2,18}... | collective-permute-start | bytes 98312 | tf_op jit(solution)/shard_map/ppermute | solution.py:443
  20.1 5.7 %copy-start.2 = (f32[4,2,3,3,2,8,128]{6,5,4,3,2,1,0:T(8,128)S(1)}, f32[4,2,3,3,2,8,128]{6,5,4,3,2,1,0:T(8,128)}, u32[]{:S(2)}) copy-start(f32[4,2,3,3,2,8,128]{6,5,4,3,2,1,0:T(8,128)} %p.1) | copy-start | bytes 1769476
  20.8 13.1 %copy-start.1 = (f32[4,2,3,3,2,8,128]{6,5,4,3,2,1,0:T(8,128)S(1)}, f32[4,2,3,3,2,8,128]{6,5,4,3,2,1,0:T(8,128)}, u32[]{:S(2)}) copy-start(f32[4,2,3,3,2,8,128]{6,5,4,3,2,1,0:T(8,128)} %v.9) | copy-start | bytes 1769476
  26.0 10.0 %collective-permute-start.6 = (f32[24,8,128]{2,1,0:T(8,128)S(1)}, f32[24,8,128]{2,1,0:T(8,128)S(1)}, u32[]{:S(2)}, u32[]{:S(2)}) collective-permute-start(f32[24,8,128]{2,1,0:T(8,128)S(1)} %get-tuple-element.40), channel_id=1, source_target_pairs={{0,192},{64,0},{128,64},{192,128},{1,193},{65,1},{129,65},{193,129... | collective-permute-start | bytes 294920 | tf_op jit(solution)/shard_map/ppermute | solution.py:443
  28.7 7.3 %collective-permute-start.8 = (f32[24,8,128]{2,1,0:T(8,128)S(1)}, f32[24,8,128]{2,1,0:T(8,128)S(1)}, u32[]{:S(2)}, u32[]{:S(2)}) collective-permute-start(f32[24,8,128]{2,1,0:T(8,128)S(1)} %get-tuple-element.42), channel_id=1, source_target_pairs={{0,15},{1,0},{2,1},{3,2},{4,3},{5,4},{6,5},{7,6},{8,7},{9,8},{10,9... | collective-permute-start | bytes 294920 | tf_op jit(solution)/shard_map/ppermute | solution.py:443
  30.6 5.4 %collective-permute-start.7 = (f32[8,8,128]{2,1,0:T(8,128)S(1)}, f32[8,8,128]{2,1,0:T(8,128)S(1)}, u32[]{:S(2)}, u32[]{:S(2)}) collective-permute-start(f32[8,8,128]{2,1,0:T(8,128)S(1)} %get-tuple-element.41), channel_id=1, source_target_pairs={{0,48},{16,0},{32,16},{48,32},{1,49},{17,1},{33,17},{49,33},{2,50}... | collective-permute-start | bytes 98312 | tf_op jit(solution)/shard_map/ppermute | solution.py:443
  37.6 20.8 %all-to-all-start = ((f32[256,1,128]{2,1,0:T(1,128)}), f32[256,1,128]{2,1,0:T(1,128)S(1)}, u32[]{:S(2)}, u32[]{:S(2)}) async-start(f32[256,1,128]{2,1,0:T(1,128)} %bitcast.1), calls=%async_computation | async-start | bytes 262144 | tf_op jit(solution)/shard_map/all_to_all | solution.py:460
  46.1 5.9 %collective-permute-start.9 = (f32[24,8,128]{2,1,0:T(8,128)S(1)}, f32[24,8,128]{2,1,0:T(8,128)S(1)}, u32[]{:S(2)}, u32[]{:S(2)}) collective-permute-start(f32[24,8,128]{2,1,0:T(8,128)S(1)} %get-tuple-element.47), channel_id=1, source_target_pairs={{0,64},{64,128},{128,192},{192,0},{1,65},{65,129},{129,193},{193,1... | collective-permute-start | bytes 294920 | tf_op jit(solution)/shard_map/ppermute | solution.py:443
  47.6 9.5 %collective-permute-start.11 = (f32[24,8,128]{2,1,0:T(8,128)S(1)}, f32[24,8,128]{2,1,0:T(8,128)S(1)}, u32[]{:S(2)}, u32[]{:S(2)}) collective-permute-start(f32[24,8,128]{2,1,0:T(8,128)S(1)} %get-tuple-element.49), channel_id=1, source_target_pairs={{0,1},{1,2},{2,3},{3,4},{4,5},{5,6},{6,7},{7,8},{8,9},{9,10},{10,1... | collective-permute-start | bytes 294920 | tf_op jit(solution)/shard_map/ppermute | solution.py:443
  48.9 3.1 %collective-permute-start.10 = (f32[8,8,128]{2,1,0:T(8,128)S(1)}, f32[8,8,128]{2,1,0:T(8,128)S(1)}, u32[]{:S(2)}, u32[]{:S(2)}) collective-permute-start(f32[8,8,128]{2,1,0:T(8,128)S(1)} %get-tuple-element.48), channel_id=1, source_target_pairs={{0,16},{16,32},{32,48},{48,0},{1,17},{17,33},{33,49},{49,1},{2,18}... | collective-permute-start | bytes 98312 | tf_op jit(solution)/shard_map/ppermute | solution.py:443
where the time goes:
time: 59.5 us; the launch traced here: 59.3 us
  starting transfers between devices  34.9 us (59%)
  waiting for transfers between devices  15 us (25%)
  Pallas kernels  7.6 us (13%)
  local copies, waits for them, and re-layouts  1.07 us (2%)
  between operations  0.72 us (1%)
    ppermute x12, starting transfers between devices, shift(): return lax.ppermute(a, axis, [(i, (i + step) % n) for i in range(n)])  27 us
    ppermute x12, waiting for transfers between devices, shift(): return lax.ppermute(a, axis, [(i, (i + step) % n) for i in range(n)])  13.7 us
    all_to_all x1, starting transfers between devices, body(): lax.all_to_all(trace, mesh.axis_names, split_axis=0, concat_axis=0, tiled...  7.92 us
    pallas_call x11, Pallas kernels, run(): pl.pallas_call(kernel, out_shape=[jax.ShapeDtypeStruct(s, F32) for s in s...  7.6 us
    all_to_all x1, waiting for transfers between devices, body(): lax.all_to_all(trace, mesh.axis_names, split_axis=0, concat_axis=0, tiled...  1.29 us
  transfers between devices with their start and end apart: 13, of which 8 were waited for; matrix products, arithmetic and copies ran while one was open for 0% of the time, Pallas kernels for 5%

commit v1 on v0

--- a/solution.py
+++ b/solution.py
@@ -432,6 +432,7 @@
 MOM = (4, 8, 2, 8, 128)
 CORNER = (6, 2, 3, 3, 2, 8, 128)
 BIG = 400_000_000
+AXES = ("gx", "gy", "zt")
 VMEM_LIMIT = 16 * 1024 * 1024
 
 
@@ -443,7 +444,10 @@
         return lax.ppermute(a, axis, [(i, (i + step) % n) for i in range(n)])
 
     def halos(arrays, step):
-        return [shift(a, axis, step) for a, axis in zip(arrays, ("gx", "gy", "zt"), strict=True)]
+        out = []
+        for a, axis in zip(arrays, AXES, strict=True):
+            out.append(shift(a, axis, step))
+        return out
 
     def body(v, p):
         halo = halos(call(pack_kernel, HALO_SHORT, 1_000_000, ((18, 8, 128),))(v), -1)

time: 59.5 us -> 59.5 us (level)
  no operation moved by 1% of the time
where the time goes in v1:
time: 59.5 us; the launch traced here: 59.3 us
  starting transfers between devices  34.9 us (59%)
  waiting for transfers between devices  15 us (25%)
  Pallas kernels  7.6 us (13%)
  local copies, waits for them, and re-layouts  1.07 us (2%)
  between operations  0.72 us (1%)
    ppermute x12, starting transfers between devices, shift(): return lax.ppermute(a, axis, [(i, (i + step) % n) for i in range(n)])  27 us
    ppermute x12, waiting for transfers between devices, shift(): return lax.ppermute(a, axis, [(i, (i + step) % n) for i in range(n)])  13.7 us
    all_to_all x1, starting transfers between devices, body(): lax.all_to_all(trace, mesh.axis_names, split_axis=0, concat_axis=0, tiled...  7.92 us
    pallas_call x11, Pallas kernels, run(): pl.pallas_call(kernel, out_shape=[jax.ShapeDtypeStruct(s, F32) for s in s...  7.6 us
    all_to_all x1, waiting for transfers between devices, body(): lax.all_to_all(trace, mesh.axis_names, split_axis=0, concat_axis=0, tiled...  1.29 us
  transfers between devices with their start and end apart: 13, of which 8 were waited for; matrix products, arithmetic and copies ran while one was open for 0% of the time, Pallas kernels for 5%

profile of v1, /device:TPU:1, one launch (start us, length us, event | category | flops | bytes accessed | tf_op | source)
XLA Modules:
  0.0 59.3 jit_solution(9913533509106394235)
XLA Ops:
  0.6 1.1 %copy-done = f32[4,2,3,3,2,8,128]{6,5,4,3,2,1,0:T(8,128)S(1)} copy-done((f32[4,2,3,3,2,8,128]{6,5,4,3,2,1,0:T(8,128)S(1)}, f32[4,2,3,3,2,8,128]{6,5,4,3,2,1,0:T(8,128)}, u32[]{:S(2)}) %copy-start) | copy-done | bytes 589848
  1.8 3.4 %collective-permute-start = (f32[42,8,128]{2,1,0:T(8,128)S(1)}, f32[42,8,128]{2,1,0:T(8,128)S(1)}, u32[]{:S(2)}, u32[]{:S(2)}) collective-permute-start(f32[42,8,128]{2,1,0:T(8,128)S(1)} %get-tuple-element.28), channel_id=1, source_target_pairs={{0,192},{64,0},{128,64},{192,128},{1,193},{65,1},{129,65},{193,129... | collective-permute-start | bytes 516104 | tf_op jit(solution)/shard_map/ppermute | solution.py:444
  5.2 8.2 %collective-permute-start.2 = (f32[42,8,128]{2,1,0:T(8,128)S(1)}, f32[42,8,128]{2,1,0:T(8,128)S(1)}, u32[]{:S(2)}, u32[]{:S(2)}) collective-permute-start(f32[42,8,128]{2,1,0:T(8,128)S(1)} %get-tuple-element.30), channel_id=1, source_target_pairs={{0,15},{1,0},{2,1},{3,2},{4,3},{5,4},{6,5},{7,6},{8,7},{9,8},{10,9... | collective-permute-start | bytes 516104 | tf_op jit(solution)/shard_map/ppermute | solution.py:444
  13.4 1.2 %collective-permute-start.1 = (f32[14,8,128]{2,1,0:T(8,128)S(1)}, f32[14,8,128]{2,1,0:T(8,128)S(1)}, u32[]{:S(2)}, u32[]{:S(2)}) collective-permute-start(f32[14,8,128]{2,1,0:T(8,128)S(1)} %get-tuple-element.29), channel_id=1, source_target_pairs={{0,48},{16,0},{32,16},{48,32},{1,49},{17,1},{33,17},{49,33},{2,50}... | collective-permute-start | bytes 172040 | tf_op jit(solution)/shard_map/ppermute | solution.py:444
  15.0 2.0 %collective-permute-done.1.yh = f32[14,8,128]{2,1,0:T(8,128)S(1)} collective-permute-done((f32[14,8,128]{2,1,0:T(8,128)S(1)}, f32[14,8,128]{2,1,0:T(8,128)S(1)}, u32[]{:S(2)}, u32[]{:S(2)}) %collective-permute-start.1) | collective-permute-done | bytes 57376 | tf_op jit(solution)/shard_map/ppermute | solution.py:444
  17.0 1.5 %shard_map.51 = (f32[4,8,2,8,128]{4,3,2,1,0:T(8,128)S(1)}, f32[24,8,128]{2,1,0:T(8,128)S(1)}, f32[8,8,128]{2,1,0:T(8,128)S(1)}, f32[24,8,128]{2,1,0:T(8,128)S(1)...) custom-call(f32[4,2,3,3,2,8,128]{6,5,4,3,2,1,0:T(8,128)S(1)} %copy-d, ...), custom_call_target="tpu_custom_call" | custom-call | flops 400000000 | bytes 2000000 | tf_op jit(solution)/shard_map/pallas_call | solution.py:415
  18.8 1.3 %collective-permute-start.4 = (f32[8,8,128]{2,1,0:T(8,128)S(1)}, f32[8,8,128]{2,1,0:T(8,128)S(1)}, u32[]{:S(2)}, u32[]{:S(2)}) collective-permute-start(f32[8,8,128]{2,1,0:T(8,128)S(1)} %get-tuple-element.34), channel_id=1, source_target_pairs={{0,16},{16,32},{32,48},{48,0},{1,17},{17,33},{33,49},{49,1},{2,18}... | collective-permute-start | bytes 98312 | tf_op jit(solution)/shard_map/ppermute | solution.py:444
  20.1 0.7 %shard_map.52.f = f32[4,8,2,8,128]{4,3,2,1,0:T(8,128)S(1)} custom-call(f32[4,2,3,3,2,8,128]{6,5,4,3,2,1,0:T(8,128)S(1)} %copy-done, f32[6,2,3,3,2,8,128]{6,5,4,3,2,1,0:T(8,128)S(1)} %get-tuple-element.31.corners, f32[4,8,2,8,128]{4,3,2,1,0:T(8,128)S(1)} %get-tuple-element.32.f), custom_call_target="tpu_custom_call" | custom-call | flops 100000000 | bytes 2000000 | tf_op jit(solution)/shard_map/pallas_call | solution.py:415
  21.1 2.2 %collective-permute-done.3.xr = f32[24,8,128]{2,1,0:T(8,128)S(1)} collective-permute-done((f32[24,8,128]{2,1,0:T(8,128)S(1)}, f32[24,8,128]{2,1,0:T(8,128)S(1)}, u32[]{:S(2)}, u32[]{:S(2)}) %collective-permute-start.3) | collective-permute-done | bytes 98336 | tf_op jit(solution)/shard_map/ppermute | solution.py:444
  23.3 2.5 %collective-permute-done.5.zr = f32[24,8,128]{2,1,0:T(8,128)S(1)} collective-permute-done((f32[24,8,128]{2,1,0:T(8,128)S(1)}, f32[24,8,128]{2,1,0:T(8,128)S(1)}, u32[]{:S(2)}, u32[]{:S(2)}) %collective-permute-start.5) | collective-permute-done | bytes 98336 | tf_op jit(solution)/shard_map/ppermute | solution.py:444
  26.0 2.7 %collective-permute-start.6 = (f32[24,8,128]{2,1,0:T(8,128)S(1)}, f32[24,8,128]{2,1,0:T(8,128)S(1)}, u32[]{:S(2)}, u32[]{:S(2)}) collective-permute-start(f32[24,8,128]{2,1,0:T(8,128)S(1)} %get-tuple-element.40), channel_id=1, source_target_pairs={{0,192},{64,0},{128,64},{192,128},{1,193},{65,1},{129,65},{193,129... | collective-permute-start | bytes 294920 | tf_op jit(solution)/shard_map/ppermute | solution.py:444
  28.7 1.9 %collective-permute-start.8 = (f32[24,8,128]{2,1,0:T(8,128)S(1)}, f32[24,8,128]{2,1,0:T(8,128)S(1)}, u32[]{:S(2)}, u32[]{:S(2)}) collective-permute-start(f32[24,8,128]{2,1,0:T(8,128)S(1)} %get-tuple-element.42), channel_id=1, source_target_pairs={{0,15},{1,0},{2,1},{3,2},{4,3},{5,4},{6,5},{7,6},{8,7},{9,8},{10,9... | collective-permute-start | bytes 294920 | tf_op jit(solution)/shard_map/ppermute | solution.py:444
  30.6 3.2 %collective-permute-start.7 = (f32[8,8,128]{2,1,0:T(8,128)S(1)}, f32[8,8,128]{2,1,0:T(8,128)S(1)}, u32[]{:S(2)}, u32[]{:S(2)}) collective-permute-start(f32[8,8,128]{2,1,0:T(8,128)S(1)} %get-tuple-element.41), channel_id=1, source_target_pairs={{0,48},{16,0},{32,16},{48,32},{1,49},{17,1},{33,17},{49,33},{2,50}... | collective-permute-start | bytes 98312 | tf_op jit(solution)/shard_map/ppermute | solution.py:444
  34.6 1.4 %collective-permute-done.7.ym = f32[8,8,128]{2,1,0:T(8,128)S(1)} collective-permute-done((f32[8,8,128]{2,1,0:T(8,128)S(1)}, f32[8,8,128]{2,1,0:T(8,128)S(1)}, u32[]{:S(2)}, u32[]{:S(2)}) %collective-permute-start.7) | collective-permute-done | bytes 32800 | tf_op jit(solution)/shard_map/ppermute | solution.py:444
  36.0 1.6 %shard_map.56 = (f32[6,2,3,3,2,8,128]{6,5,4,3,2,1,0:T(8,128)S(1)}, f32[256,128]{1,0:T(8,128)}) custom-call(f32[4,2,3,3,2,8,128]{6,5,4,3,2,1,0:T(8,128)S(1)} %shard_map.54.v, f32[6,2,3,3,2,8,128]{6,5,4,3,2,1,0:T(8,128)S(1)} %shard_map.55.a, f32[54,8,128]{2,1,0:T(8,128)S(1)} %get-tuple-element.37.xh, f32[18,8,128]{2,1,0:T(8,128)S(1)} %get-tuple-element.38.yh, ...), custom_call_target="tpu_custom_call" | custom-call | flops 100000000 | bytes 2000000 | tf_op jit(solution)/shard_map/pallas_call | solution.py:415
  37.6 7.9 %all-to-all-start = ((f32[256,1,128]{2,1,0:T(1,128)}), f32[256,1,128]{2,1,0:T(1,128)S(1)}, u32[]{:S(2)}, u32[]{:S(2)}) async-start(f32[256,1,128]{2,1,0:T(1,128)} %bitcast.1), calls=%async_computation | async-start | bytes 262144 | tf_op jit(solution)/shard_map/all_to_all | solution.py:464
  45.5 0.6 %shard_map.57 = (f32[4,8,2,8,128]{4,3,2,1,0:T(8,128)S(1)}, f32[24,8,128]{2,1,0:T(8,128)S(1)}, f32[8,8,128]{2,1,0:T(8,128)S(1)}, f32[24,8,128]{2,1,0:T(8,128)S(1)}) custom-call(f32[6,2,3,3,2,8,128]{6,5,4,3,2,1,0:T(8,128)S(1)} %shard_map.55.a, f32[6,2,3,3,2,8,128]{6,5,4,3,2,1,0:T(8,128)S(1)} %get-tuple-element.43.corners), custom_call_target="tpu_custom_call" | custom-call | flops 100000000 | bytes 2000000 | tf_op jit(solution)/shard_map/pallas_call | solution.py:415
  46.1 1.4 %collective-permute-start.9 = (f32[24,8,128]{2,1,0:T(8,128)S(1)}, f32[24,8,128]{2,1,0:T(8,128)S(1)}, u32[]{:S(2)}, u32[]{:S(2)}) collective-permute-start(f32[24,8,128]{2,1,0:T(8,128)S(1)} %get-tuple-element.47), channel_id=1, source_target_pairs={{0,64},{64,128},{128,192},{192,0},{1,65},{65,129},{129,193},{193,1... | collective-permute-start | bytes 294920 | tf_op jit(solution)/shard_map/ppermute | solution.py:444
  47.6 1.3 %collective-permute-start.11 = (f32[24,8,128]{2,1,0:T(8,128)S(1)}, f32[24,8,128]{2,1,0:T(8,128)S(1)}, u32[]{:S(2)}, u32[]{:S(2)}) collective-permute-start(f32[24,8,128]{2,1,0:T(8,128)S(1)} %get-tuple-element.49), channel_id=1, source_target_pairs={{0,1},{1,2},{2,3},{3,4},{4,5},{5,6},{6,7},{7,8},{8,9},{9,10},{10,1... | collective-permute-start | bytes 294920 | tf_op jit(solution)/shard_map/ppermute | solution.py:444
  48.9 2.1 %collective-permute-start.10 = (f32[8,8,128]{2,1,0:T(8,128)S(1)}, f32[8,8,128]{2,1,0:T(8,128)S(1)}, u32[]{:S(2)}, u32[]{:S(2)}) collective-permute-start(f32[8,8,128]{2,1,0:T(8,128)S(1)} %get-tuple-element.48), channel_id=1, source_target_pairs={{0,16},{16,32},{32,48},{48,0},{1,17},{17,33},{33,49},{49,1},{2,18}... | collective-permute-start | bytes 98312 | tf_op jit(solution)/shard_map/ppermute | solution.py:444
  51.0 0.9 %shard_map.58 = (f32[4,8,2,8,128]{4,3,2,1,0:T(8,128)S(1)}, f32[4,2,3,3,2,8,128]{6,5,4,3,2,1,0:T(8,128)}) custom-call(f32[4,2,3,3,2,8,128]{6,5,4,3,2,1,0:T(8,128)S(1)} %shard_map.54.v, f32[6,2,3,3,2,8,128]{6,5,4,3,2,1,0:T(8,128)S(1)} %get-tuple-element.43.corners, f32[4,8,2,8,128]{4,3,2,1,0:T(8,128)S(1)} %get-tuple-element.44.f), custom_call_target="tpu_custom_call" | custom-call | flops 100000000 | bytes 2000000 | tf_op jit(solution)/shard_map/pallas_call | solution.py:415
  52.0 5.1 %collective-permute-done.11.zr = f32[24,8,128]{2,1,0:T(8,128)S(1)} collective-permute-done((f32[24,8,128]{2,1,0:T(8,128)S(1)}, f32[24,8,128]{2,1,0:T(8,128)S(1)}, u32[]{:S(2)}, u32[]{:S(2)}) %collective-permute-start.11) | collective-permute-done | bytes 98336 | tf_op jit(solution)/shard_map/ppermute | solution.py:444
  57.1 1.3 %all-to-all-done = f32[256,1,128]{2,1,0:T(1,128)S(1)} async-done(((f32[256,1,128]{2,1,0:T(1,128)}), f32[256,1,128]{2,1,0:T(1,128)S(1)}, u32[]{:S(2)}, u32[]{:S(2)}) %all-to-all-start) | async-done | bytes 131104 | tf_op jit(solution)/shard_map/all_to_all | solution.py:464
  58.4 0.9 %shard_map.59 = (f32[4,2,3,3,2,8,128]{6,5,4,3,2,1,0:T(8,128)}, f32[1,1]{1,0:T(1,128)}) custom-call(f32[4,8,2,8,128]{4,3,2,1,0:T(8,128)S(1)} %get-tuple-element.36.h, f32[4,8,2,8,128]{4,3,2,1,0:T(8,128)S(1)} %get-tuple-element.46.f, f32[24,8,128]{2,1,0:T(8,128)S(1)} %collective-permute-done.9.xr, f32[8,8,128]{2,1,0:T(8,128)S(1)} %collective-permute-done.10.yr, ...), custom_call_target="tpu_custom_call" | custom-call | flops 1000000 | bytes 2000000 | tf_op jit(solution)/shard_map/pallas_call | solution.py:415
  (19 shorter events, 2.1 us)
Async XLA Ops:
  0.6 1.1 %copy-start = (f32[4,2,3,3,2,8,128]{6,5,4,3,2,1,0:T(8,128)S(1)}, f32[4,2,3,3,2,8,128]{6,5,4,3,2,1,0:T(8,128)}, u32[]{:S(2)}) copy-start(f32[4,2,3,3,2,8,128]{6,5,4,3,2,1,0:T(8,128)} %v.9) | copy-start | bytes 1769476
  1.8 15.2 %collective-permute-start = (f32[42,8,128]{2,1,0:T(8,128)S(1)}, f32[42,8,128]{2,1,0:T(8,128)S(1)}, u32[]{:S(2)}, u32[]{:S(2)}) collective-permute-start(f32[42,8,128]{2,1,0:T(8,128)S(1)} %get-tuple-element.28), channel_id=1, source_target_pairs={{0,192},{64,0},{128,64},{192,128},{1,193},{65,1},{129,65},{193,129... | collective-permute-start | bytes 516104 | tf_op jit(solution)/shard_map/ppermute | solution.py:444
  5.2 11.8 %collective-permute-start.2 = (f32[42,8,128]{2,1,0:T(8,128)S(1)}, f32[42,8,128]{2,1,0:T(8,128)S(1)}, u32[]{:S(2)}, u32[]{:S(2)}) collective-permute-start(f32[42,8,128]{2,1,0:T(8,128)S(1)} %get-tuple-element.30), channel_id=1, source_target_pairs={{0,15},{1,0},{2,1},{3,2},{4,3},{5,4},{6,5},{7,6},{8,7},{9,8},{10,9... | collective-permute-start | bytes 516104 | tf_op jit(solution)/shard_map/ppermute | solution.py:444
  13.4 3.6 %collective-permute-start.1 = (f32[14,8,128]{2,1,0:T(8,128)S(1)}, f32[14,8,128]{2,1,0:T(8,128)S(1)}, u32[]{:S(2)}, u32[]{:S(2)}) collective-permute-start(f32[14,8,128]{2,1,0:T(8,128)S(1)} %get-tuple-element.29), channel_id=1, source_target_pairs={{0,48},{16,0},{32,16},{48,32},{1,49},{17,1},{33,17},{49,33},{2,50}... | collective-permute-start | bytes 172040 | tf_op jit(solution)/shard_map/ppermute | solution.py:444
  18.6 4.8 %collective-permute-start.3 = (f32[24,8,128]{2,1,0:T(8,128)S(1)}, f32[24,8,128]{2,1,0:T(8,128)S(1)}, u32[]{:S(2)}, u32[]{:S(2)}) collective-permute-start(f32[24,8,128]{2,1,0:T(8,128)S(1)} %get-tuple-element.33), channel_id=1, source_target_pairs={{0,64},{64,128},{128,192},{192,0},{1,65},{65,129},{129,193},{193,1... | collective-permute-start | bytes 294920 | tf_op jit(solution)/shard_map/ppermute | solution.py:444
  18.7 7.2 %collective-permute-start.5 = (f32[24,8,128]{2,1,0:T(8,128)S(1)}, f32[24,8,128]{2,1,0:T(8,128)S(1)}, u32[]{:S(2)}, u32[]{:S(2)}) collective-permute-start(f32[24,8,128]{2,1,0:T(8,128)S(1)} %get-tuple-element.35), channel_id=1, source_target_pairs={{0,1},{1,2},{2,3},{3,4},{4,5},{5,6},{6,7},{7,8},{8,9},{9,10},{10,1... | collective-permute-start | bytes 294920 | tf_op jit(solution)/shard_map/ppermute | solution.py:444
  18.8 2.4 %collective-permute-start.4 = (f32[8,8,128]{2,1,0:T(8,128)S(1)}, f32[8,8,128]{2,1,0:T(8,128)S(1)}, u32[]{:S(2)}, u32[]{:S(2)}) collective-permute-start(f32[8,8,128]{2,1,0:T(8,128)S(1)} %get-tuple-element.34), channel_id=1, source_target_pairs={{0,16},{16,32},{32,48},{48,0},{1,17},{17,33},{33,49},{49,1},{2,18}... | collective-permute-start | bytes 98312 | tf_op jit(solution)/shard_map/ppermute | solution.py:444
  20.1 5.7 %copy-start.2 = (f32[4,2,3,3,2,8,128]{6,5,4,3,2,1,0:T(8,128)S(1)}, f32[4,2,3,3,2,8,128]{6,5,4,3,2,1,0:T(8,128)}, u32[]{:S(2)}) copy-start(f32[4,2,3,3,2,8,128]{6,5,4,3,2,1,0:T(8,128)} %p.1) | copy-start | bytes 1769476
  20.8 13.1 %copy-start.1 = (f32[4,2,3,3,2,8,128]{6,5,4,3,2,1,0:T(8,128)S(1)}, f32[4,2,3,3,2,8,128]{6,5,4,3,2,1,0:T(8,128)}, u32[]{:S(2)}) copy-start(f32[4,2,3,3,2,8,128]{6,5,4,3,2,1,0:T(8,128)} %v.9) | copy-start | bytes 1769476
  26.0 10.0 %collective-permute-start.6 = (f32[24,8,128]{2,1,0:T(8,128)S(1)}, f32[24,8,128]{2,1,0:T(8,128)S(1)}, u32[]{:S(2)}, u32[]{:S(2)}) collective-permute-start(f32[24,8,128]{2,1,0:T(8,128)S(1)} %get-tuple-element.40), channel_id=1, source_target_pairs={{0,192},{64,0},{128,64},{192,128},{1,193},{65,1},{129,65},{193,129... | collective-permute-start | bytes 294920 | tf_op jit(solution)/shard_map/ppermute | solution.py:444
  28.7 7.3 %collective-permute-start.8 = (f32[24,8,128]{2,1,0:T(8,128)S(1)}, f32[24,8,128]{2,1,0:T(8,128)S(1)}, u32[]{:S(2)}, u32[]{:S(2)}) collective-permute-start(f32[24,8,128]{2,1,0:T(8,128)S(1)} %get-tuple-element.42), channel_id=1, source_target_pairs={{0,15},{1,0},{2,1},{3,2},{4,3},{5,4},{6,5},{7,6},{8,7},{9,8},{10,9... | collective-permute-start | bytes 294920 | tf_op jit(solution)/shard_map/ppermute | solution.py:444
  30.6 5.4 %collective-permute-start.7 = (f32[8,8,128]{2,1,0:T(8,128)S(1)}, f32[8,8,128]{2,1,0:T(8,128)S(1)}, u32[]{:S(2)}, u32[]{:S(2)}) collective-permute-start(f32[8,8,128]{2,1,0:T(8,128)S(1)} %get-tuple-element.41), channel_id=1, source_target_pairs={{0,48},{16,0},{32,16},{48,32},{1,49},{17,1},{33,17},{49,33},{2,50}... | collective-permute-start | bytes 98312 | tf_op jit(solution)/shard_map/ppermute | solution.py:444
  37.6 20.8 %all-to-all-start = ((f32[256,1,128]{2,1,0:T(1,128)}), f32[256,1,128]{2,1,0:T(1,128)S(1)}, u32[]{:S(2)}, u32[]{:S(2)}) async-start(f32[256,1,128]{2,1,0:T(1,128)} %bitcast.1), calls=%async_computation | async-start | bytes 262144 | tf_op jit(solution)/shard_map/all_to_all | solution.py:464
  46.1 5.9 %collective-permute-start.9 = (f32[24,8,128]{2,1,0:T(8,128)S(1)}, f32[24,8,128]{2,1,0:T(8,128)S(1)}, u32[]{:S(2)}, u32[]{:S(2)}) collective-permute-start(f32[24,8,128]{2,1,0:T(8,128)S(1)} %get-tuple-element.47), channel_id=1, source_target_pairs={{0,64},{64,128},{128,192},{192,0},{1,65},{65,129},{129,193},{193,1... | collective-permute-start | bytes 294920 | tf_op jit(solution)/shard_map/ppermute | solution.py:444
  47.6 9.5 %collective-permute-start.11 = (f32[24,8,128]{2,1,0:T(8,128)S(1)}, f32[24,8,128]{2,1,0:T(8,128)S(1)}, u32[]{:S(2)}, u32[]{:S(2)}) collective-permute-start(f32[24,8,128]{2,1,0:T(8,128)S(1)} %get-tuple-element.49), channel_id=1, source_target_pairs={{0,1},{1,2},{2,3},{3,4},{4,5},{5,6},{6,7},{7,8},{8,9},{9,10},{10,1... | collective-permute-start | bytes 294920 | tf_op jit(solution)/shard_map/ppermute | solution.py:444
  48.9 3.1 %collective-permute-start.10 = (f32[8,8,128]{2,1,0:T(8,128)S(1)}, f32[8,8,128]{2,1,0:T(8,128)S(1)}, u32[]{:S(2)}, u32[]{:S(2)}) collective-permute-start(f32[8,8,128]{2,1,0:T(8,128)S(1)} %get-tuple-element.48), channel_id=1, source_target_pairs={{0,16},{16,32},{32,48},{48,0},{1,17},{17,33},{33,49},{49,1},{2,18}... | collective-permute-start | bytes 98312 | tf_op jit(solution)/shard_map/ppermute | solution.py:444

commit v2 on v1

--- a/solution.py
+++ b/solution.py
@@ -283,7 +283,7 @@
     for m, n in PAIRS:
         for x in range(2):
             vm, vn = load_link(links, m, x), load_link(links, n, x)
-            t = traceless(product(product(vm, load_pair(corners, m, n, x)), vn, bh=True))
+            t = traceless(product(product(vm, load_pair(corners(m, n), m, n, x)), vn, bh=True))
             for c in range(8):
                 out[m, c, x] = out[m, c, x] + t[c]
                 out[n, c, x] = out[n, c, x] - t[c]
@@ -294,22 +294,43 @@
         ys[c, 6:8, :] = jnp.zeros((2, 128), F32)
 
 
-def force_kernel(v, a, xh, yh, zh, f, xs, ys, zs, xw, yw, zw, corners):
-    clear_rows(ys)
-    for short, whole, count in ((xh, xw, 3), (yh, yw, 1), (zh, zw, 3)):
-        for k in range(count):
+def early_kernel(v, a, xh, zh, f, xs, zs, xw, zw, corners):
+    for short, whole in ((xh, xw), (zh, zw)):
+        for k in range(3):
             store_flat(whole, 18 * k, load_short(short, 14 * k))
-    ahead = Ahead(v, xw, yw, zw)
-    force = Force(f, xs, ys, zs)
-    for m, n in PAIRS:
+    ahead = Ahead(v, xw, None, zw)
+    force = Force(f, xs, None, zs)
+    for m, n in PAIRS:
+        if 1 in (m, n):
+            continue
         for x in range(2):
             c = corner(ahead, m, n, x)
             store_pair(corners, m, n, x, c)
             add_shifted(force, load_pair(a, m, n, x), m, n, x, c)
 
 
-def upper_kernel(v, corners, f, out):
-    add_upper(v, corners, f, out)
+def late_kernel(v, a, xw, zw, yh, f1, xs1, zs1, f, xs, ys, zs, yw, corners):
+    clear_rows(ys)
+    store_flat(yw, 0, load_short(yh, 0))
+    force = Force(f, xs, ys, zs)
+    for m in others(1):
+        f[m] = f1[m]
+        force.seen |= {(m, c, x) for c in range(8) for x in range(2)}
+        for d, new, old in ((0, xs, xs1), (2, zs, zs1)):
+            if m != d:
+                new[8 * slot(d, m) : 8 * slot(d, m) + 8] = old[8 * slot(d, m) : 8 * slot(d, m) + 8]
+    ahead = Ahead(v, xw, yw, zw)
+    for m, n in PAIRS:
+        if 1 not in (m, n):
+            continue
+        for x in range(2):
+            c = corner(ahead, m, n, x)
+            store_pair(corners, m, n, x, c)
+            add_shifted(force, load_pair(a, m, n, x), m, n, x, c)
+
+
+def upper_kernel(v, early, late, f, out):
+    add_upper(v, lambda m, n: late if 1 in (m, n) else early, f, out)
 
 
 def arrived(xr, yr, zr, m, c, x):
@@ -390,7 +411,7 @@
 
 def final_kernel(v, corners, f, out, links):
     links[...] = v[...]
-    add_upper(v, corners, f, out)
+    add_upper(v, lambda m, n: corners, f, out)
 
 
 def last_kernel(h, f, xr, yr, zr, traces, out, plaquette):
@@ -431,7 +452,6 @@
 HALO_MOM = ((24, 8, 128), (8, 8, 128), (24, 8, 128))
 MOM = (4, 8, 2, 8, 128)
 CORNER = (6, 2, 3, 3, 2, 8, 128)
-BIG = 400_000_000
 AXES = ("gx", "gy", "zt")
 VMEM_LIMIT = 16 * 1024 * 1024
 
@@ -452,10 +472,14 @@
     def body(v, p):
         halo = halos(call(pack_kernel, HALO_SHORT, 1_000_000, ((18, 8, 128),))(v), -1)
         (a,) = call(local_kernel, (CORNER,), 100_000_000)(v)
-        f, *up = call(force_kernel, (MOM, *HALO_MOM, *HALO_LINK, CORNER), BIG)(v, a, *halo)
-        up, halo, corners = up[:3], up[3:6], up[6]
+        xh, yh, zh = halo
+        shapes = (MOM, HALO_MOM[0], HALO_MOM[2], HALO_LINK[0], HALO_LINK[2], CORNER)
+        f, xs, zs, xh, zh, early = call(early_kernel, shapes, 100_000_000)(v, a, xh, zh)
+        shapes = (MOM, *HALO_MOM, HALO_LINK[1], CORNER)
+        f, *up, yh, late = call(late_kernel, shapes, 100_000_000)(v, a, xh, zh, yh, f, xs, zs)
+        halo = (xh, yh, zh)
         up = halos(up, 1)
-        (f,) = call(upper_kernel, (MOM,), 100_000_000)(v, corners, f)
+        (f,) = call(upper_kernel, (MOM,), 100_000_000)(v, early, late, f)
         h, *down = call(half_kernel, (MOM, *HALO_MOM), 1_000_000)(p, f, *up)
         down = halos(down, -1)
         (new,) = call(link_kernel, (LINK,), 100_000_000)(v, h)

time: 59.5 us -> 59.5 us (level)
  waiting for transfers between devices: 15 us -> 14.1 us
  starting transfers between devices: 34.9 us -> 35.8 us
    ppermute x12, waiting for transfers between devices: 13.7 us -> 12.8 us  [shift(): return lax.ppermute(a, axis, [(i, (i + step) % n) for i in range(n)])]
    ppermute x12, starting transfers between devices: 27 us -> 27.9 us  [shift(): return lax.ppermute(a, axis, [(i, (i + step) % n) for i in range(n)])]
    pallas_call x11 -> x12, Pallas kernels: 7.6 us -> 7.55 us  [run(): pl.pallas_call(kernel, out_shape=[jax.ShapeDtypeStruct(s, F32) for s in s...]
  transfers between devices with their start and end apart: 13 -> 13, of which waited for: 8 -> 8; matrix products, arithmetic and copies ran while one was open for 0% -> 0% of each run, Pallas kernels for 5% -> 7%
where the time goes in v2:
time: 59.5 us; the launch traced here: 59.3 us
  starting transfers between devices  35.8 us (60%)
  waiting for transfers between devices  14.1 us (24%)
  Pallas kernels  7.55 us (13%)
  local copies, waits for them, and re-layouts  1.07 us (2%)
  between operations  0.73 us (1%)
    ppermute x12, starting transfers between devices, shift(): return lax.ppermute(a, axis, [(i, (i + step) % n) for i in range(n)])  27.9 us
    ppermute x12, waiting for transfers between devices, shift(): return lax.ppermute(a, axis, [(i, (i + step) % n) for i in range(n)])  12.8 us
    all_to_all x1, starting transfers between devices, body(): lax.all_to_all(trace, mesh.axis_names, split_axis=0, concat_axis=0, tiled...  7.92 us
    pallas_call x12, Pallas kernels, run(): pl.pallas_call(kernel, out_shape=[jax.ShapeDtypeStruct(s, F32) for s in s...  7.55 us
    all_to_all x1, waiting for transfers between devices, body(): lax.all_to_all(trace, mesh.axis_names, split_axis=0, concat_axis=0, tiled...  1.29 us
  transfers between devices with their start and end apart: 13, of which 8 were waited for; matrix products, arithmetic and copies ran while one was open for 0% of the time, Pallas kernels for 7%

profile of v2, /device:TPU:1, one launch (start us, length us, event | category | flops | bytes accessed | tf_op | source)
XLA Modules:
  0.0 59.3 jit_solution(1930409157774167651)
XLA Ops:
  0.6 1.1 %copy-done = f32[4,2,3,3,2,8,128]{6,5,4,3,2,1,0:T(8,128)S(1)} copy-done((f32[4,2,3,3,2,8,128]{6,5,4,3,2,1,0:T(8,128)S(1)}, f32[4,2,3,3,2,8,128]{6,5,4,3,2,1,0:T(8,128)}, u32[]{:S(2)}) %copy-start) | copy-done | bytes 589848
  1.8 3.4 %collective-permute-start = (f32[42,8,128]{2,1,0:T(8,128)S(1)}, f32[42,8,128]{2,1,0:T(8,128)S(1)}, u32[]{:S(2)}, u32[]{:S(2)}) collective-permute-start(f32[42,8,128]{2,1,0:T(8,128)S(1)} %get-tuple-element.32), channel_id=1, source_target_pairs={{0,192},{64,0},{128,64},{192,128},{1,193},{65,1},{129,65},{193,129... | collective-permute-start | bytes 516104 | tf_op jit(solution)/shard_map/ppermute | solution.py:464
  5.2 8.2 %collective-permute-start.1 = (f32[42,8,128]{2,1,0:T(8,128)S(1)}, f32[42,8,128]{2,1,0:T(8,128)S(1)}, u32[]{:S(2)}, u32[]{:S(2)}) collective-permute-start(f32[42,8,128]{2,1,0:T(8,128)S(1)} %get-tuple-element.33), channel_id=1, source_target_pairs={{0,15},{1,0},{2,1},{3,2},{4,3},{5,4},{6,5},{7,6},{8,7},{9,8},{10,9... | collective-permute-start | bytes 516104 | tf_op jit(solution)/shard_map/ppermute | solution.py:464
  13.4 1.2 %collective-permute-start.2 = (f32[14,8,128]{2,1,0:T(8,128)S(1)}, f32[14,8,128]{2,1,0:T(8,128)S(1)}, u32[]{:S(2)}, u32[]{:S(2)}) collective-permute-start(f32[14,8,128]{2,1,0:T(8,128)S(1)} %get-tuple-element.37), channel_id=1, source_target_pairs={{0,48},{16,0},{32,16},{48,32},{1,49},{17,1},{33,17},{49,33},{2,50}... | collective-permute-start | bytes 172040 | tf_op jit(solution)/shard_map/ppermute | solution.py:464
  15.0 1.2 %collective-permute-done.1.zh = f32[42,8,128]{2,1,0:T(8,128)S(1)} collective-permute-done((f32[42,8,128]{2,1,0:T(8,128)S(1)}, f32[42,8,128]{2,1,0:T(8,128)S(1)}, u32[]{:S(2)}, u32[]{:S(2)}) %collective-permute-start.1) | collective-permute-done | bytes 172064 | tf_op jit(solution)/shard_map/ppermute | solution.py:464
  16.2 0.9 %shard_map.51 = (f32[4,8,2,8,128]{4,3,2,1,0:T(8,128)S(1)}, f32[24,8,128]{2,1,0:T(8,128)S(1)}, f32[24,8,128]{2,1,0:T(8,128)S(1)}, f32[54,8,128]{2,1,0:T(8,128)S(1...) custom-call(f32[4,2,3,3,2,8,128]{6,5,4,3,2,1,0:T(8,128)S(1)} %copy-done, ...), custom_call_target="tpu_custom_call" | custom-call | flops 100000000 | bytes 2000000 | tf_op jit(solution)/shard_map/pallas_call | solution.py:436
  17.1 0.6 %shard_map.52 = (f32[4,8,2,8,128]{4,3,2,1,0:T(8,128)S(1)}, f32[24,8,128]{2,1,0:T(8,128)S(1)}, f32[8,8,128]{2,1,0:T(8,128)S(1)}, f32[24,8,128]{2,1,0:T(8,128)S(1)...) custom-call(f32[4,2,3,3,2,8,128]{6,5,4,3,2,1,0:T(8,128)S(1)} %copy-done, ...), custom_call_target="tpu_custom_call" | custom-call | flops 100000000 | bytes 2000000 | tf_op jit(solution)/shard_map/pallas_call | solution.py:436
  17.9 2.2 %collective-permute-start.4 = (f32[8,8,128]{2,1,0:T(8,128)S(1)}, f32[8,8,128]{2,1,0:T(8,128)S(1)}, u32[]{:S(2)}, u32[]{:S(2)}) collective-permute-start(f32[8,8,128]{2,1,0:T(8,128)S(1)} %get-tuple-element.44), channel_id=1, source_target_pairs={{0,16},{16,32},{32,48},{48,0},{1,17},{17,33},{33,49},{49,1},{2,18}... | collective-permute-start | bytes 98312 | tf_op jit(solution)/shard_map/ppermute | solution.py:464
  20.1 0.7 %shard_map.53.f = f32[4,8,2,8,128]{4,3,2,1,0:T(8,128)S(1)} custom-call(f32[4,2,3,3,2,8,128]{6,5,4,3,2,1,0:T(8,128)S(1)} %copy-done, f32[6,2,3,3,2,8,128]{6,5,4,3,2,1,0:T(8,128)S(1)} %get-tuple-element.34.early, f32[6,2,3,3,2,8,128]{6,5,4,3,2,1,0:T(8,128)S(1)} %get-tuple-element.41.late, f32[4,8,2,8,128]{4,3,2,1,0:T(8,128)S(1)} %get-tuple-element.42.f), custom_call_target="tpu_custom_call" | custom-call | flops 100000000 | bytes 2000000 | tf_op jit(solution)/shard_map/pallas_call | solution.py:436
  21.1 1.4 %collective-permute-done.3.xr = f32[24,8,128]{2,1,0:T(8,128)S(1)} collective-permute-done((f32[24,8,128]{2,1,0:T(8,128)S(1)}, f32[24,8,128]{2,1,0:T(8,128)S(1)}, u32[]{:S(2)}, u32[]{:S(2)}) %collective-permute-start.3) | collective-permute-done | bytes 98336 | tf_op jit(solution)/shard_map/ppermute | solution.py:464
  22.5 3.2 %collective-permute-done.5.zr = f32[24,8,128]{2,1,0:T(8,128)S(1)} collective-permute-done((f32[24,8,128]{2,1,0:T(8,128)S(1)}, f32[24,8,128]{2,1,0:T(8,128)S(1)}, u32[]{:S(2)}, u32[]{:S(2)}) %collective-permute-start.5) | collective-permute-done | bytes 98336 | tf_op jit(solution)/shard_map/ppermute | solution.py:464
  25.9 2.7 %collective-permute-start.6 = (f32[24,8,128]{2,1,0:T(8,128)S(1)}, f32[24,8,128]{2,1,0:T(8,128)S(1)}, u32[]{:S(2)}, u32[]{:S(2)}) collective-permute-start(f32[24,8,128]{2,1,0:T(8,128)S(1)} %get-tuple-element.48), channel_id=1, source_target_pairs={{0,192},{64,0},{128,64},{192,128},{1,193},{65,1},{129,65},{193,129... | collective-permute-start | bytes 294920 | tf_op jit(solution)/shard_map/ppermute | solution.py:464
  28.5 2.0 %collective-permute-start.8 = (f32[24,8,128]{2,1,0:T(8,128)S(1)}, f32[24,8,128]{2,1,0:T(8,128)S(1)}, u32[]{:S(2)}, u32[]{:S(2)}) collective-permute-start(f32[24,8,128]{2,1,0:T(8,128)S(1)} %get-tuple-element.50), channel_id=1, source_target_pairs={{0,15},{1,0},{2,1},{3,2},{4,3},{5,4},{6,5},{7,6},{8,7},{9,8},{10,9... | collective-permute-start | bytes 294920 | tf_op jit(solution)/shard_map/ppermute | solution.py:464
  30.6 3.2 %collective-permute-start.7 = (f32[8,8,128]{2,1,0:T(8,128)S(1)}, f32[8,8,128]{2,1,0:T(8,128)S(1)}, u32[]{:S(2)}, u32[]{:S(2)}) collective-permute-start(f32[8,8,128]{2,1,0:T(8,128)S(1)} %get-tuple-element.49), channel_id=1, source_target_pairs={{0,48},{16,0},{32,16},{48,32},{1,49},{17,1},{33,17},{49,33},{2,50}... | collective-permute-start | bytes 98312 | tf_op jit(solution)/shard_map/ppermute | solution.py:464
  34.6 1.4 %collective-permute-done.7.ym = f32[8,8,128]{2,1,0:T(8,128)S(1)} collective-permute-done((f32[8,8,128]{2,1,0:T(8,128)S(1)}, f32[8,8,128]{2,1,0:T(8,128)S(1)}, u32[]{:S(2)}, u32[]{:S(2)}) %collective-permute-start.7) | collective-permute-done | bytes 32800 | tf_op jit(solution)/shard_map/ppermute | solution.py:464
  36.0 1.6 %shard_map.57 = (f32[6,2,3,3,2,8,128]{6,5,4,3,2,1,0:T(8,128)S(1)}, f32[256,128]{1,0:T(8,128)}) custom-call(f32[4,2,3,3,2,8,128]{6,5,4,3,2,1,0:T(8,128)S(1)} %shard_map.55.v, f32[6,2,3,3,2,8,128]{6,5,4,3,2,1,0:T(8,128)S(1)} %shard_map.56.a, f32[54,8,128]{2,1,0:T(8,128)S(1)} %get-tuple-element.35.xw.xh, f32[18,8,128]{2,1,0:T(8,128)S(1)} %get-tuple-element.47.yh, ...), custom_call_target="tpu_custom_call" | custom-call | flops 100000000 | bytes 2000000 | tf_op jit(solution)/shard_map/pallas_call | solution.py:436
  37.6 7.9 %all-to-all-start = ((f32[256,1,128]{2,1,0:T(1,128)}), f32[256,1,128]{2,1,0:T(1,128)S(1)}, u32[]{:S(2)}, u32[]{:S(2)}) async-start(f32[256,1,128]{2,1,0:T(1,128)} %bitcast.1), calls=%async_computation | async-start | bytes 262144 | tf_op jit(solution)/shard_map/all_to_all | solution.py:488
  46.1 1.4 %collective-permute-start.9 = (f32[24,8,128]{2,1,0:T(8,128)S(1)}, f32[24,8,128]{2,1,0:T(8,128)S(1)}, u32[]{:S(2)}, u32[]{:S(2)}) collective-permute-start(f32[24,8,128]{2,1,0:T(8,128)S(1)} %get-tuple-element.55), channel_id=1, source_target_pairs={{0,64},{64,128},{128,192},{192,0},{1,65},{65,129},{129,193},{193,1... | collective-permute-start | bytes 294920 | tf_op jit(solution)/shard_map/ppermute | solution.py:464
  47.5 1.3 %collective-permute-start.11 = (f32[24,8,128]{2,1,0:T(8,128)S(1)}, f32[24,8,128]{2,1,0:T(8,128)S(1)}, u32[]{:S(2)}, u32[]{:S(2)}) collective-permute-start(f32[24,8,128]{2,1,0:T(8,128)S(1)} %get-tuple-element.57), channel_id=1, source_target_pairs={{0,1},{1,2},{2,3},{3,4},{4,5},{5,6},{6,7},{7,8},{8,9},{9,10},{10,1... | collective-permute-start | bytes 294920 | tf_op jit(solution)/shard_map/ppermute | solution.py:464
  48.9 2.1 %collective-permute-start.10 = (f32[8,8,128]{2,1,0:T(8,128)S(1)}, f32[8,8,128]{2,1,0:T(8,128)S(1)}, u32[]{:S(2)}, u32[]{:S(2)}) collective-permute-start(f32[8,8,128]{2,1,0:T(8,128)S(1)} %get-tuple-element.56), channel_id=1, source_target_pairs={{0,16},{16,32},{32,48},{48,0},{1,17},{17,33},{33,49},{49,1},{2,18}... | collective-permute-start | bytes 98312 | tf_op jit(solution)/shard_map/ppermute | solution.py:464
  51.0 0.9 %shard_map.59 = (f32[4,8,2,8,128]{4,3,2,1,0:T(8,128)S(1)}, f32[4,2,3,3,2,8,128]{6,5,4,3,2,1,0:T(8,128)}) custom-call(f32[4,2,3,3,2,8,128]{6,5,4,3,2,1,0:T(8,128)S(1)} %shard_map.55.v, f32[6,2,3,3,2,8,128]{6,5,4,3,2,1,0:T(8,128)S(1)} %get-tuple-element.51.corners, f32[4,8,2,8,128]{4,3,2,1,0:T(8,128)S(1)} %get-tuple-element.52.f), custom_call_target="tpu_custom_call" | custom-call | flops 100000000 | bytes 2000000 | tf_op jit(solution)/shard_map/pallas_call | solution.py:436
  52.0 5.1 %collective-permute-done.11.zr = f32[24,8,128]{2,1,0:T(8,128)S(1)} collective-permute-done((f32[24,8,128]{2,1,0:T(8,128)S(1)}, f32[24,8,128]{2,1,0:T(8,128)S(1)}, u32[]{:S(2)}, u32[]{:S(2)}) %collective-permute-start.11) | collective-permute-done | bytes 98336 | tf_op jit(solution)/shard_map/ppermute | solution.py:464
  57.1 1.3 %all-to-all-done = f32[256,1,128]{2,1,0:T(1,128)S(1)} async-done(((f32[256,1,128]{2,1,0:T(1,128)}), f32[256,1,128]{2,1,0:T(1,128)S(1)}, u32[]{:S(2)}, u32[]{:S(2)}) %all-to-all-start) | async-done | bytes 131104 | tf_op jit(solution)/shard_map/all_to_all | solution.py:488
  58.3 0.9 %shard_map.60 = (f32[4,2,3,3,2,8,128]{6,5,4,3,2,1,0:T(8,128)}, f32[1,1]{1,0:T(1,128)}) custom-call(f32[4,8,2,8,128]{4,3,2,1,0:T(8,128)S(1)} %get-tuple-element.46.h, f32[4,8,2,8,128]{4,3,2,1,0:T(8,128)S(1)} %get-tuple-element.54.f, f32[24,8,128]{2,1,0:T(8,128)S(1)} %collective-permute-done.9.xr, f32[8,8,128]{2,1,0:T(8,128)S(1)} %collective-permute-done.10.yr, ...), custom_call_target="tpu_custom_call" | custom-call | flops 1000000 | bytes 2000000 | tf_op jit(solution)/shard_map/pallas_call | solution.py:436
  (20 shorter events, 2.7 us)
Async XLA Ops:
  0.6 1.1 %copy-start = (f32[4,2,3,3,2,8,128]{6,5,4,3,2,1,0:T(8,128)S(1)}, f32[4,2,3,3,2,8,128]{6,5,4,3,2,1,0:T(8,128)}, u32[]{:S(2)}) copy-start(f32[4,2,3,3,2,8,128]{6,5,4,3,2,1,0:T(8,128)} %v.11) | copy-start | bytes 1769476
  1.8 13.1 %collective-permute-start = (f32[42,8,128]{2,1,0:T(8,128)S(1)}, f32[42,8,128]{2,1,0:T(8,128)S(1)}, u32[]{:S(2)}, u32[]{:S(2)}) collective-permute-start(f32[42,8,128]{2,1,0:T(8,128)S(1)} %get-tuple-element.32), channel_id=1, source_target_pairs={{0,192},{64,0},{128,64},{192,128},{1,193},{65,1},{129,65},{193,129... | collective-permute-start | bytes 516104 | tf_op jit(solution)/shard_map/ppermute | solution.py:464
  5.2 11.0 %collective-permute-start.1 = (f32[42,8,128]{2,1,0:T(8,128)S(1)}, f32[42,8,128]{2,1,0:T(8,128)S(1)}, u32[]{:S(2)}, u32[]{:S(2)}) collective-permute-start(f32[42,8,128]{2,1,0:T(8,128)S(1)} %get-tuple-element.33), channel_id=1, source_target_pairs={{0,15},{1,0},{2,1},{3,2},{4,3},{5,4},{6,5},{7,6},{8,7},{9,8},{10,9... | collective-permute-start | bytes 516104 | tf_op jit(solution)/shard_map/ppermute | solution.py:464
  13.4 3.7 %collective-permute-start.2 = (f32[14,8,128]{2,1,0:T(8,128)S(1)}, f32[14,8,128]{2,1,0:T(8,128)S(1)}, u32[]{:S(2)}, u32[]{:S(2)}) collective-permute-start(f32[14,8,128]{2,1,0:T(8,128)S(1)} %get-tuple-element.37), channel_id=1, source_target_pairs={{0,48},{16,0},{32,16},{48,32},{1,49},{17,1},{33,17},{49,33},{2,50}... | collective-permute-start | bytes 172040 | tf_op jit(solution)/shard_map/ppermute | solution.py:464
  17.7 4.8 %collective-permute-start.3 = (f32[24,8,128]{2,1,0:T(8,128)S(1)}, f32[24,8,128]{2,1,0:T(8,128)S(1)}, u32[]{:S(2)}, u32[]{:S(2)}) collective-permute-start(f32[24,8,128]{2,1,0:T(8,128)S(1)} %get-tuple-element.43), channel_id=1, source_target_pairs={{0,64},{64,128},{128,192},{192,0},{1,65},{65,129},{129,193},{193,1... | collective-permute-start | bytes 294920 | tf_op jit(solution)/shard_map/ppermute | solution.py:464
  17.8 7.9 %collective-permute-start.5 = (f32[24,8,128]{2,1,0:T(8,128)S(1)}, f32[24,8,128]{2,1,0:T(8,128)S(1)}, u32[]{:S(2)}, u32[]{:S(2)}) collective-permute-start(f32[24,8,128]{2,1,0:T(8,128)S(1)} %get-tuple-element.45), channel_id=1, source_target_pairs={{0,1},{1,2},{2,3},{3,4},{4,5},{5,6},{6,7},{7,8},{8,9},{9,10},{10,1... | collective-permute-start | bytes 294920 | tf_op jit(solution)/shard_map/ppermute | solution.py:464
  17.9 3.2 %collective-permute-start.4 = (f32[8,8,128]{2,1,0:T(8,128)S(1)}, f32[8,8,128]{2,1,0:T(8,128)S(1)}, u32[]{:S(2)}, u32[]{:S(2)}) collective-permute-start(f32[8,8,128]{2,1,0:T(8,128)S(1)} %get-tuple-element.44), channel_id=1, source_target_pairs={{0,16},{16,32},{32,48},{48,0},{1,17},{17,33},{33,49},{49,1},{2,18}... | collective-permute-start | bytes 98312 | tf_op jit(solution)/shard_map/ppermute | solution.py:464
  20.1 5.6 %copy-start.2 = (f32[4,2,3,3,2,8,128]{6,5,4,3,2,1,0:T(8,128)S(1)}, f32[4,2,3,3,2,8,128]{6,5,4,3,2,1,0:T(8,128)}, u32[]{:S(2)}) copy-start(f32[4,2,3,3,2,8,128]{6,5,4,3,2,1,0:T(8,128)} %p.1) | copy-start | bytes 1769476
  20.7 13.1 %copy-start.1 = (f32[4,2,3,3,2,8,128]{6,5,4,3,2,1,0:T(8,128)S(1)}, f32[4,2,3,3,2,8,128]{6,5,4,3,2,1,0:T(8,128)}, u32[]{:S(2)}) copy-start(f32[4,2,3,3,2,8,128]{6,5,4,3,2,1,0:T(8,128)} %v.11) | copy-start | bytes 1769476
  25.9 10.1 %collective-permute-start.6 = (f32[24,8,128]{2,1,0:T(8,128)S(1)}, f32[24,8,128]{2,1,0:T(8,128)S(1)}, u32[]{:S(2)}, u32[]{:S(2)}) collective-permute-start(f32[24,8,128]{2,1,0:T(8,128)S(1)} %get-tuple-element.48), channel_id=1, source_target_pairs={{0,192},{64,0},{128,64},{192,128},{1,193},{65,1},{129,65},{193,129... | collective-permute-start | bytes 294920 | tf_op jit(solution)/shard_map/ppermute | solution.py:464
  28.5 7.4 %collective-permute-start.8 = (f32[24,8,128]{2,1,0:T(8,128)S(1)}, f32[24,8,128]{2,1,0:T(8,128)S(1)}, u32[]{:S(2)}, u32[]{:S(2)}) collective-permute-start(f32[24,8,128]{2,1,0:T(8,128)S(1)} %get-tuple-element.50), channel_id=1, source_target_pairs={{0,15},{1,0},{2,1},{3,2},{4,3},{5,4},{6,5},{7,6},{8,7},{9,8},{10,9... | collective-permute-start | bytes 294920 | tf_op jit(solution)/shard_map/ppermute | solution.py:464
  30.6 5.4 %collective-permute-start.7 = (f32[8,8,128]{2,1,0:T(8,128)S(1)}, f32[8,8,128]{2,1,0:T(8,128)S(1)}, u32[]{:S(2)}, u32[]{:S(2)}) collective-permute-start(f32[8,8,128]{2,1,0:T(8,128)S(1)} %get-tuple-element.49), channel_id=1, source_target_pairs={{0,48},{16,0},{32,16},{48,32},{1,49},{17,1},{33,17},{49,33},{2,50}... | collective-permute-start | bytes 98312 | tf_op jit(solution)/shard_map/ppermute | solution.py:464
  37.6 20.8 %all-to-all-start = ((f32[256,1,128]{2,1,0:T(1,128)}), f32[256,1,128]{2,1,0:T(1,128)S(1)}, u32[]{:S(2)}, u32[]{:S(2)}) async-start(f32[256,1,128]{2,1,0:T(1,128)} %bitcast.1), calls=%async_computation | async-start | bytes 262144 | tf_op jit(solution)/shard_map/all_to_all | solution.py:488
  46.1 5.9 %collective-permute-start.9 = (f32[24,8,128]{2,1,0:T(8,128)S(1)}, f32[24,8,128]{2,1,0:T(8,128)S(1)}, u32[]{:S(2)}, u32[]{:S(2)}) collective-permute-start(f32[24,8,128]{2,1,0:T(8,128)S(1)} %get-tuple-element.55), channel_id=1, source_target_pairs={{0,64},{64,128},{128,192},{192,0},{1,65},{65,129},{129,193},{193,1... | collective-permute-start | bytes 294920 | tf_op jit(solution)/shard_map/ppermute | solution.py:464
  47.5 9.5 %collective-permute-start.11 = (f32[24,8,128]{2,1,0:T(8,128)S(1)}, f32[24,8,128]{2,1,0:T(8,128)S(1)}, u32[]{:S(2)}, u32[]{:S(2)}) collective-permute-start(f32[24,8,128]{2,1,0:T(8,128)S(1)} %get-tuple-element.57), channel_id=1, source_target_pairs={{0,1},{1,2},{2,3},{3,4},{4,5},{5,6},{6,7},{7,8},{8,9},{9,10},{10,1... | collective-permute-start | bytes 294920 | tf_op jit(solution)/shard_map/ppermute | solution.py:464
  48.9 3.1 %collective-permute-start.10 = (f32[8,8,128]{2,1,0:T(8,128)S(1)}, f32[8,8,128]{2,1,0:T(8,128)S(1)}, u32[]{:S(2)}, u32[]{:S(2)}) collective-permute-start(f32[8,8,128]{2,1,0:T(8,128)S(1)} %get-tuple-element.56), channel_id=1, source_target_pairs={{0,16},{16,32},{32,48},{48,0},{1,17},{17,33},{33,49},{49,1},{2,18}... | collective-permute-start | bytes 98312 | tf_op jit(solution)/shard_map/ppermute | solution.py:464
